TPU v7x, 256 devices: a 4x2x16 block of a 4x16x16 slice. The times are simulated.
256 devices in a mesh: rep: 2 (over y), seq: 128 (over z, x, core).
Axes of the slice: x: 4, y: 2, z: 16, core: 2. Of those that a mesh axis runs over, the one named last changes fastest.
The devices are a block of a 4x16x16 slice.
Arguments:
- latents: bfloat16 [16, 196608], P(None, ('rep', 'seq')), parts along dimension 1, may hold values from -6 to 6
- layout: int32 [256, 768], P('rep'), parts along dimension 0, may hold values from 0 to 98303, as said below
- assign: int32 [16], P('rep'), parts along dimension 0, may hold values from 0 to 7, as said below
- counts: int32 [16], P('rep'), parts along dimension 0, may hold values from 1 to 3
- latent_cache: bfloat16 [2, 1024, 1024], P(None, ('rep', 'seq')), parts along dimension 1, may hold values from -6 to 6
- feature_cache: bfloat16 [2, 1024, 64, 384], P(None, ('rep', 'seq')), parts along dimension 1, may hold values from -4 to 4
- first_weight: bfloat16 [3, 3, 3, 16, 384], replicated, may hold values from -0.3125 to 0.3125
- first_bias: float32 [384], replicated, may hold values from -3 to 3
- norm_gain: float32 [384], replicated, may hold values from 0.25 to 1.75
- second_weight: bfloat16 [3, 3, 3, 384, 192], replicated, may hold values from -0.0625 to 0.0625
- second_bias: float32 [192], replicated, may hold values from -3 to 3
Outputs:
- decoded_frames: bfloat16 [3, 2048, 128, 192], P(None, ('rep', 'seq')), parts along dimension 1
- latent_cache_next: bfloat16 [2, 1024, 1024], P(None, ('rep', 'seq')), parts along dimension 1
- feature_cache_next: bfloat16 [2, 1024, 64, 384], P(None, ('rep', 'seq')), parts along dimension 1
There are 2 independent parts, one for each index of `rep`. A program takes and returns all parts, laid end to end along the dimension named above; an argument that names none is the same for every part. Nothing has to cross between parts.
Inputs may be any that keep to these rules, and one draw needn't show every extreme that they name: assign is a permutation of 0 to 7. layout is a permutation of 0 to 98303. Call the cells of request assign[g], rows k * 4 to (k + 1) * 4 - 1, all frames and columns, the tile of seq index (g * 16 + k - 8) mod 128; every row of layout holds exactly 6 cells of every tile.
All inputs are finite; a program needn't handle non-finite values.
Results may differ from a plain program's by a relative error of at most 0.0034.
Values may be sent and summed in bfloat16 or wider, within the bound.
No kernel may reach another device: no remote copies, remote signals or barrier semaphores. Data moves between devices by JAX's collectives and lax.ppermute only.
A program may use at most 128 MiB of HBM per device.

v0:
```python
import jax
import jax.numpy as jnp
from jax import lax
from jax.sharding import PartitionSpec as P

LAT_CH = 16
REQS = 8
FMAX = 3
ROWS_DEV = 4
W = 64


def padded_2(array, sides, width):
    for axis, dim in sides:
        devices, length = (lax.axis_size(axis), array.shape[dim])
        up = [(i, (i + 1) % devices) for i in range(devices)]
        down = [(j, i) for i, j in up]
        last = lax.slice_in_dim(array, length - width, length, axis=dim)
        first = lax.slice_in_dim(array, 0, width, axis=dim)
        before = lax.ppermute(last, axis, up)
        after = lax.ppermute(first, axis, down)
        array = jnp.concatenate([before, array, after], axis=dim)
    return array


def tile_numbers(layout, assign, per_group, devices):
    height = ROWS_DEV * per_group
    offset = per_group // 2
    tile_cells = FMAX * ROWS_DEV * W
    column = layout % W
    remain = layout // W
    image_row = remain % height
    remain = remain // height
    frame_index = remain % FMAX
    request = remain // FMAX
    group_ranks = jnp.arange(REQS, dtype=jnp.int32)
    group_index = jnp.sum(jnp.where(assign == request[..., None], group_ranks, 0), axis=-1)
    place = group_index * per_group + image_row // ROWS_DEV
    target = (place - offset + devices) % devices
    within = (frame_index * ROWS_DEV + image_row % ROWS_DEV) * W + column
    return target * tile_cells + within


def keep_rows(values, rim_width, position, height):
    row_index = position * ROWS_DEV - rim_width + jnp.arange(values.shape[1], dtype=jnp.int32)
    inside = (row_index >= 0) & (row_index < height)
    return jnp.where(inside[None, :, None, None], values, jnp.zeros((), values.dtype))


def causal_conv(values, weight, offset):
    result = lax.conv_general_dilated(
        values[None],
        weight,
        (1, 1, 1),
        ((0, 0), (0, 0), (1, 1)),
        dimension_numbers=("NDHWC", "DHWIO", "NDHWC"),
        preferred_element_type=jnp.float32,
    )
    return result[0] + offset


def activate(linear, norm_gain):
    inverse = lax.rsqrt(jnp.mean(linear * linear, axis=-1, keepdims=True) + 1e-06)
    return jax.nn.silu(linear * inverse * norm_gain).astype(jnp.bfloat16)


def body(
    latents,
    layout,
    assign,
    counts,
    latent_cache,
    feature_cache,
    first_weight,
    first_bias,
    norm_gain,
    second_weight,
    second_bias,
):
    devices = lax.axis_size("seq")
    myself = lax.axis_index("seq")
    per_group = devices // REQS
    offset = per_group // 2
    height = ROWS_DEV * per_group
    tile_cells = FMAX * ROWS_DEV * W
    per_peer = tile_cells // devices
    numbers = tile_numbers(layout, assign, per_group, devices)
    own_numbers = lax.dynamic_index_in_dim(numbers, myself, 0, keepdims=False)
    sending_order = jnp.argsort(own_numbers)
    outgoing = jnp.take(latents, sending_order, axis=1).reshape(LAT_CH, devices, per_peer)
    incoming = lax.all_to_all(outgoing, "seq", split_axis=1, concat_axis=1, tiled=True)
    arrived = lax.dynamic_slice_in_dim(jnp.sort(numbers, axis=1), myself * per_peer, per_peer, 1)
    placing = jnp.argsort((arrived - myself * tile_cells).reshape(-1))
    arranged = jnp.take(incoming.reshape(LAT_CH, tile_cells), placing, axis=1)
    window = jnp.transpose(arranged.reshape(LAT_CH, FMAX, ROWS_DEV, W), (1, 2, 3, 0))
    place = (myself + offset) % devices
    position = place % per_group
    request = jnp.take(assign, place // per_group)
    live_frames = jnp.take(counts, request)
    first_input = jnp.concatenate([latent_cache.reshape(2, ROWS_DEV, W, LAT_CH), window], axis=0)
    padded = keep_rows(padded_2(first_input, (("seq", 1),), 2), 2, position, height)
    widened = activate(causal_conv(padded, first_weight, first_bias), norm_gain)
    cached = padded_2(feature_cache, (("seq", 1),), 1)
    extended = keep_rows(jnp.concatenate([cached, widened], axis=0), 1, position, height)
    second_input = extended[:, 1:-1]
    doubled = jnp.repeat(jnp.repeat(extended, 2, axis=1)[:, 1:-1], 2, axis=2)
    decoded = causal_conv(doubled, second_weight, second_bias)
    frame_index = jnp.arange(FMAX, dtype=jnp.int32)[:, None, None, None]
    decoded_frames = jnp.where(frame_index < live_frames, decoded, 0.0).astype(jnp.bfloat16)
    latent_next = lax.dynamic_slice_in_dim(first_input, live_frames, 2, 0).reshape(
        2, ROWS_DEV, W * LAT_CH
    )
    feature_next = lax.dynamic_slice_in_dim(second_input, live_frames, 2, 0)
    return (decoded_frames, latent_next, feature_next)


def solution(mesh):
    return jax.shard_map(
        body,
        mesh=mesh,
        in_specs=(
            P(None, ("rep", "seq")),
            P("rep", None),
            P("rep"),
            P("rep"),
            P(None, ("rep", "seq"), None),
            P(None, ("rep", "seq"), None, None),
            P(),
            P(),
            P(),
            P(),
            P(),
        ),
        out_specs=(
            P(None, ("rep", "seq"), None, None),
            P(None, ("rep", "seq"), None),
            P(None, ("rep", "seq"), None, None),
        ),
        check_vma=False,
    )
```

profile of v0, /device:TPU:40, one launch (start us, length us, event | category | flops | bytes accessed | tf_op | source)
XLA Modules:
  0.0 162.3 jit_solution(7621123937541215728)
XLA Ops:
  7.2 0.0 copy-start
  7.2 0.1 sort.43.cloned.1.call-start
  7.3 1.8 %add_select_fusion.6 = s32[128,768]{1,0:T(8,128)S(1)} fusion(s32[128,768]{1,0:T(8,128)} %param.14), kind=kLoop, calls=%fused_computation.42 | loop fusion | flops 3735552 | bytes 786432 | tf_op jit(solution)/shard_map/jit(floor_divide)/jit(_where)/select_n | solution.py:35
  9.1 0.0 copy-start.10
  9.1 1.8 %select_reduce_fusion = s32[128,768]{1,0:T(8,128)S(1)} fusion(s32[128,768]{1,0:T(8,128)S(1)} %add_select_fusion.6, s32[8]{0:T(128)} %param.15), kind=kLoop, calls=%fused_computation.14 | loop fusion | flops 2260992 | bytes 786464 | tf_op jit(solution)/shard_map/reduce_sum | solution.py:37
  10.9 3.2 %fusion.28 = s32[128,768]{1,0:T(8,128)} fusion(s32[128,768]{1,0:T(8,128)S(1)} %select_reduce_fusion, s32[128,768]{1,0:T(8,128)} %param.14), kind=kLoop, calls=%fused_computation.56 | loop fusion | flops 8159232 | bytes 1179648 | tf_op jit(solution)/shard_map/add | solution.py:41
  14.1 0.1 sort.43.cloned.1.call-update
  14.1 0.8 dynamic-slice_reduce_fusion
  14.9 4.4 %sort.39 = (s32[768]{0:T(1024)}, s32[768]{0:T(1024)S(1)}) sort(s32[768]{0:T(1024)S(1)} %dynamic-slice_reduce_fusion, s32[768]{0:T(1024)S(1)} %iota.27), dimensions={0}, to_apply=%region_1.2 | sort | flops 7680 | bytes 12288 | tf_op jit(solution)/shard_map/jit(argsort)/sort | solution.py:89
  19.3 0.2 copy.86
  19.5 1.9 %gather_fusion = bf16[768,16]{1,0:T(8,128)(2,1)S(1)} fusion(bf16[16,768]{0,1:T(8,128)(2,1)S(1)} %copy.86, s32[1024]{0:T(1024)S(1)} %pad_clamp_fusion.1), kind=kCustom, calls=%fused_computation.clone | custom fusion | bytes 52224 | tf_op jit(solution)/shard_map/jit(_take)/gather | solution.py:90
  21.4 0.2 select_bitcast_fusion.1
  21.6 0.8 reshape.109
  22.3 32.2 %all-to-all-start = ((bf16[16,128,6]{0,2,1:T(8,128)(2,1)}), bf16[16,128,6]{0,2,1:T(8,128)(2,1)S(1)}, u32[]{:S(2)}, u32[]{:S(2)}) async-start(bf16[16,128,6]{0,2,1:T(8,128)(2,1)} %reshape.109), calls=%async_computation | async-start | bytes 524288 | tf_op jit(solution)/shard_map/all_to_all | solution.py:91
  54.5 0.3 copy.83
  54.8 1.0 fusion.49
  55.8 5.1 %collective-permute-start.1 = (bf16[2,1,64,384]{3,1,2,0:T(2,128)(2,1)}, bf16[2,1,64,384]{3,1,2,0:T(2,128)(2,1)}, u32[]{:S(2)}, u32[]{:S(2)}) collective-permute-start(bf16[2,1,64,384]{3,1,2,0:T(2,128)(2,1)} %get-tuple-element.46), channel_id=1, source_target_pairs={{1,0},{2,1},{3,2},{4,3},{5,4},{6,5},{7,6},{8,7},{9,8},{10,9},{11,1... | collective-permute-start | bytes 294920 | tf_op jit(solution)/shard_map/ppermute | solution.py:21
  60.9 0.7 dynamic-slice.4
  62.3 0.7 dynamic-slice.5
  63.7 0.1 reshape.108
  63.8 0.1 copy.88
  64.0 9.0 %all-to-all-done = bf16[16,128,6]{0,2,1:T(8,128)(2,1)S(1)} async-done(((bf16[16,128,6]{0,2,1:T(8,128)(2,1)}), bf16[16,128,6]{0,2,1:T(8,128)(2,1)S(1)}, u32[]{:S(2)}, u32[]{:S(2)}) %all-to-all-start) | async-done | bytes 24608 | tf_op jit(solution)/shard_map/all_to_all | solution.py:91
  73.0 0.1 reshape.110
  73.1 0.0 sort.43.cloned.1.call-done
  73.2 1.0 dynamic-slice_subtract_fusion
  74.2 0.1 reshape.111
  74.3 4.4 %sort.41 = (s32[768]{0:T(1024)}, s32[768]{0:T(1024)S(1)}) sort(s32[768]{0:T(1024)S(1)} %reshape.111, s32[768]{0:T(1024)S(1)} %iota.28), dimensions={0}, to_apply=%region_3.5 | sort | flops 7680 | bytes 12288 | tf_op jit(solution)/shard_map/jit(argsort)/sort | solution.py:93
  78.7 1.9 %gather_fusion.1 = bf16[768,16]{1,0:T(8,128)(2,1)S(1)} fusion(bf16[16,768]{0,1:T(8,128)(2,1)S(1)} %reshape.110, s32[1024]{0:T(1024)S(1)} %pad_clamp_fusion), kind=kCustom, calls=%fused_computation.1.clone | custom fusion | bytes 52224 | tf_op jit(solution)/shard_map/jit(_take)/gather | solution.py:94
  80.6 0.2 broadcast_select_fusion
  80.8 0.1 copy.87
  81.0 0.1 collective-permute-start.2
  81.1 5.0 %collective-permute-start.3 = (bf16[5,2,64,16]{2,3,1,0:T(8,128)(2,1)S(1)}, bf16[5,2,64,16]{2,3,1,0:T(8,128)(2,1)S(1)}, u32[]{:S(2)}, u32[]{:S(2)}) collective-permute-start(bf16[5,2,64,16]{2,3,1,0:T(8,128)(2,1)S(1)} %get-tuple-element.48), channel_id=1, source_target_pairs={{1,0},{2,1},{3,2},{4,3},{5,4},{6,5},{7,6},{8,7},{9,8},{10,9},{11,1... | collective-permute-start | bytes 61448 | tf_op jit(solution)/shard_map/ppermute | solution.py:21
  86.2 0.0 copy-start.12
  86.2 0.1 copy.99
  86.3 0.8 reshape.114
  87.1 0.7 collective-permute-done.2
  87.9 0.4 copy.89
  88.3 0.1 select_bitcast_fusion
  88.4 0.1 pad.4
  88.5 0.1 copy.91
  88.7 1.8 %convolution_select_fusion = f32[3,6,8,9,384]{4,2,3,1,0:T(8,128)S(1)} fusion(bf16[3,3,3,16,384]{4,3,2,1,0:T(8,128)(2,1)S(1)} %copy-done, pred[8,9]{0,1:T(8,128)(4,1)S(1)} %copy-done.12, bf16[5,8,1,7,2,16]{5,3,4,1,0,2:T(8,128)(2,1)S(1)} %slice.48, bf16[5,8,1,8,9,16]{5,3,4,1,0,2:T(8,128)(2,1)S(1)} %copy.91), kind=kOutput, calls=%fused_computation.24 | convolution fusion | flops 430817280 | bytes 2432584 | tf_op jit(solution)/shard_map/conv_general_dilated | solution.py:51
  90.6 0.5 copy.92
  91.1 0.2 copy-done.5
  91.2 0.4 multiply_reduce_fusion
  91.6 0.1 copy.93
  91.7 0.1 copy.94
  91.8 0.7 multiply_convert_fusion
  92.6 2.0 %maximum_select_fusion = bf16[5,6,64,384]{3,1,2,0:T(8,128)(2,1)S(1)} fusion(bf16[3,6,64,384]{3,1,2,0:T(8,128)(2,1)S(1)} %multiply_convert_fusion, bf16[2,1,64,384]{3,1,2,0:T(2,128)(2,1)} %collective-permute-done.1, bf16[2,4,64,384]{3,1,2,0:T(4,128)(2,1)S(1)} %copy.83, bf16[2,1,64,384]{3,1,2,0:T(2,128)(2,1)} %collective-permute-done, ...), kind=kLoop, calls=%fused_computation.20 | loop fusion | flops 6635520 | bytes 2949126 | tf_op jit(solution)/shard_map/jit(_where)/select_n | solution.py:47
  94.7 0.5 slice.53
  95.2 0.3 copy.95
  95.5 0.1 constant_dynamic-slice_fusion
  95.6 0.8 copy.101
  96.4 0.5 broadcast_in_dim.85
  96.9 0.3 slice.50
  97.2 4.4 %broadcast_in_dim.86 = bf16[5,10,64,2,384]{4,3,2,1,0:T(2,128)(2,1)} broadcast(bf16[5,10,64,384]{3,2,1,0:T(8,128)(2,1)S(1)} %slice.50), dimensions={0,1,2,4} | broadcast | bytes 7372800 | tf_op jit(solution)/shard_map/broadcast_in_dim | solution.py:106
  101.6 11.0 %reshape.191 = bf16[5,10,1,128,384]{4,3,1,0,2:T(8,128)(2,1)} reshape(bf16[5,10,64,2,384]{4,3,2,1,0:T(2,128)(2,1)} %broadcast_in_dim.86) | data formatting | bytes 9830400 | tf_op jit(solution)/shard_map/broadcast_in_dim;reshape | solution.py:52
  112.6 7.3 %pad.6 = bf16[5,10,1,136,384]{4,3,1,0,2:T(8,128)(2,1)} pad(bf16[5,10,1,128,384]{4,3,1,0,2:T(8,128)(2,1)} %reshape.191, bf16[]{:T(256)} %constant.179.clone.1), padding=0_0x0_0x0_0x1_7x0_0 | pad | bytes 10137602 | tf_op jit(solution)/shard_map/broadcast_in_dim;reshape | solution.py:52
  119.9 8.9 %reshape.166 = bf16[5,10,1,8,17,384]{5,4,3,1,0,2:T(8,128)(2,1)} reshape(bf16[5,10,1,136,384]{4,3,1,0,2:T(8,128)(2,1)} %pad.6) | data formatting | bytes 10444800 | tf_op jit(solution)/shard_map/conv_general_dilated | solution.py:51
  128.8 4.1 %copy.97 = bf16[5,10,1,8,17,384]{5,3,4,1,0,2:T(8,128)(2,1)S(1)} copy(bf16[5,10,1,8,17,384]{5,4,3,1,0,2:T(8,128)(2,1)} %reshape.166) | data formatting | bytes 10444800 | tf_op jit(solution)/shard_map/conv_general_dilated | solution.py:51
  133.0 0.2 slice.51
  133.2 18.6 %fusion.13 = f32[3,8,8,17,192]{4,2,3,1,0:T(8,128)S(1)} fusion(bf16[3,3,3,384,192]{3,4,2,1,0:T(8,128)(2,1)S(1)} %copy-done.9, bf16[5,10,1,7,2,384]{5,3,4,1,0,2:T(8,128)(2,1)S(1)} %slice.51, bf16[5,10,1,8,17,384]{5,3,4,1,0,2:T(8,128)(2,1)S(1)} %copy.97, pred[8,17]{0,1:T(8,128)(4,1)S(1)} %copy-done.11), kind=kOutput, calls=%fused_computation.21 | convolution fusion | flops 13013139456 | bytes 12248200 | tf_op jit(solution)/shard_map/conv_general_dilated | solution.py:51
  151.8 1.1 copy.98
  152.9 0.6 fusion.10
  153.6 1.8 %copy.100 = bf16[3,8,128,192]{2,3,1,0:T(8,128)(2,1)} copy(bf16[3,8,128,192]{3,1,2,0:T(8,128)(2,1)S(1)} %fusion.10) | data formatting | bytes 2359296
  (43 shorter events, 0.3 us)
Async XLA Ops:
  7.2 81.5 %copy-start = (bf16[3,3,3,16,384]{4,3,2,1,0:T(8,128)(2,1)S(1)}, bf16[3,3,3,16,384]{4,3,2,1,0:T(8,128)(2,1)}, u32[]{:S(2)}) copy-start(bf16[3,3,3,16,384]{4,3,2,1,0:T(8,128)(2,1)} %param.19) | copy-start | bytes 995332
  7.2 12.1 %copy-start.3 = (bf16[16,768]{1,0:T(8,128)(2,1)S(1)}, bf16[16,768]{1,0:T(8,128)(2,1)}, u32[]{:S(2)}) copy-start(bf16[16,768]{1,0:T(8,128)(2,1)} %param.13) | copy-start | bytes 73732
  7.2 47.3 %copy-start.2 = (bf16[2,4,64,384]{3,2,1,0:T(8,128)(2,1)S(1)}, bf16[2,4,64,384]{3,2,1,0:T(8,128)(2,1)}, u32[]{:S(2)}) copy-start(bf16[2,4,64,384]{3,2,1,0:T(8,128)(2,1)} %param.18) | copy-start | bytes 1179652
  7.2 65.9 %sort.43.cloned.1.call-start = ((), (), s32[]{:S(2)}) async-start(), calls=%async_computation.1 | async-start | bytes 1179680 | tf_op jit(solution)/shard_map/jit(sort)/sort | solution.py:92
  9.1 51.9 %copy-start.8 = (s32[8]{0:T(128)S(1)}, s32[8]{0:T(128)}, u32[]{:S(2)}) copy-start(s32[8]{0:T(128)} %param.15) | copy-start | bytes 100
  9.1 53.2 %copy-start.10 = (s32[8]{0:T(128)S(1)}, s32[8]{0:T(128)}, u32[]{:S(2)}) copy-start(s32[8]{0:T(128)} %param.16) | copy-start | bytes 100
  9.1 54.6 %copy-start.4 = (bf16[2,4,1024]{2,1,0:T(4,128)(2,1)S(1)}, bf16[2,4,1024]{2,1,0:T(4,128)(2,1)}, u32[]{:S(2)}) copy-start(bf16[2,4,1024]{2,1,0:T(4,128)(2,1)} %param.17) | copy-start | bytes 49156
  22.3 50.7 %all-to-all-start = ((bf16[16,128,6]{0,2,1:T(8,128)(2,1)}), bf16[16,128,6]{0,2,1:T(8,128)(2,1)S(1)}, u32[]{:S(2)}, u32[]{:S(2)}) async-start(bf16[16,128,6]{0,2,1:T(8,128)(2,1)} %reshape.109), calls=%async_computation | async-start | bytes 524288 | tf_op jit(solution)/shard_map/all_to_all | solution.py:91
  55.8 36.8 %collective-permute-start = (bf16[2,1,64,384]{3,1,2,0:T(2,128)(2,1)}, bf16[2,1,64,384]{3,1,2,0:T(2,128)(2,1)}, u32[]{:S(2)}, u32[]{:S(2)}) collective-permute-start(bf16[2,1,64,384]{3,1,2,0:T(2,128)(2,1)} %get-tuple-element.45), channel_id=1, source_target_pairs={{0,1},{1,2},{2,3},{3,4},{4,5},{5,6},{6,7},{7,8},{8,9},{9,10},{10,1... | collective-permute-start | bytes 294920 | tf_op jit(solution)/shard_map/ppermute | solution.py:20
  55.8 36.8 %collective-permute-start.1 = (bf16[2,1,64,384]{3,1,2,0:T(2,128)(2,1)}, bf16[2,1,64,384]{3,1,2,0:T(2,128)(2,1)}, u32[]{:S(2)}, u32[]{:S(2)}) collective-permute-start(bf16[2,1,64,384]{3,1,2,0:T(2,128)(2,1)} %get-tuple-element.46), channel_id=1, source_target_pairs={{1,0},{2,1},{3,2},{4,3},{5,4},{6,5},{7,6},{8,7},{9,8},{10,9},{11,1... | collective-permute-start | bytes 294920 | tf_op jit(solution)/shard_map/ppermute | solution.py:21
  81.0 6.9 %collective-permute-start.2 = (bf16[5,2,64,16]{2,3,1,0:T(8,128)(2,1)S(1)}, bf16[5,2,64,16]{2,3,1,0:T(8,128)(2,1)S(1)}, u32[]{:S(2)}, u32[]{:S(2)}) collective-permute-start(bf16[5,2,64,16]{2,3,1,0:T(8,128)(2,1)S(1)} %get-tuple-element.47), channel_id=1, source_target_pairs={{0,1},{1,2},{2,3},{3,4},{4,5},{5,6},{6,7},{7,8},{8,9},{9,10},{10,1... | collective-permute-start | bytes 61448 | tf_op jit(solution)/shard_map/ppermute | solution.py:20
  81.1 6.7 %collective-permute-start.3 = (bf16[5,2,64,16]{2,3,1,0:T(8,128)(2,1)S(1)}, bf16[5,2,64,16]{2,3,1,0:T(8,128)(2,1)S(1)}, u32[]{:S(2)}, u32[]{:S(2)}) collective-permute-start(bf16[5,2,64,16]{2,3,1,0:T(8,128)(2,1)S(1)} %get-tuple-element.48), channel_id=1, source_target_pairs={{1,0},{2,1},{3,2},{4,3},{5,4},{6,5},{7,6},{8,7},{9,8},{10,9},{11,1... | collective-permute-start | bytes 61448 | tf_op jit(solution)/shard_map/ppermute | solution.py:21
  86.2 2.5 %copy-start.12 = (pred[8,9]{0,1:T(8,128)(4,1)S(1)}, pred[8,9]{0,1:T(8,128)(4,1)}, u32[]{:S(2)}) copy-start(pred[8,9]{0,1:T(8,128)(4,1)} %constant.232) | copy-start | bytes 220
  90.5 0.7 copy-start.5
  90.6 1.3 copy-start.6
  128.8 4.3 %copy-start.9 = (bf16[3,3,3,384,192]{3,4,2,1,0:T(8,128)(2,1)S(1)}, bf16[3,3,3,384,192]{3,4,2,1,0:T(8,128)(2,1)}, u32[]{:S(2)}) copy-start(bf16[3,3,3,384,192]{3,4,2,1,0:T(8,128)(2,1)} %param.22) | copy-start | bytes 11943940
  128.8 4.3 %copy-start.11 = (pred[8,17]{0,1:T(8,128)(4,1)S(1)}, pred[8,17]{0,1:T(8,128)(4,1)}, u32[]{:S(2)}) copy-start(pred[8,17]{0,1:T(8,128)(4,1)} %constant.231) | copy-start | bytes 412
  151.8 1.1 copy-start.7
  152.9 2.5 %copy-start.1 = (bf16[3,3,3,16,384]{4,3,2,1,0:T(8,128)(2,1)S(1)}, bf16[3,3,3,16,384]{4,3,2,1,0:T(8,128)(2,1)}, u32[]{:S(2)}) copy-start(bf16[3,3,3,16,384]{4,3,2,1,0:T(8,128)(2,1)} %param.19) | copy-start | bytes 995332
Sparse Core Ops, SparseCore 0:
  14.3 15.0 sort.45.cloned.1.call-done
  (1 shorter events, 0.0 us)
where the time goes:
time: 164 us; the launch traced here: 162 us
  local copies, waits for them, and re-layouts  52.7 us (32%)
  starting transfers between devices  42.4 us (26%)
  other arithmetic  20.9 us (13%)
  matrix products  20.5 us (12%)
  between operations  16 us (10%)
  waiting for transfers between devices  9.77 us (6%)
    all_to_all x1, starting transfers between devices, body(): lax.all_to_all(outgoing, 'seq', split_axis=1, concat_axis=1, tiled=True)  32.2 us
    conv_general_dilated x2, matrix products, causal_conv(): lax.conv_general_dilated(values[None], weight, (1, 1, 1), ((0, 0), (0, 0)...  20.5 us
    another operation x2, local copies, waits for them, and re-layouts, causal_conv(): values[None]  18.3 us
    conv_general_dilated x7, local copies, waits for them, and re-layouts, causal_conv(): lax.conv_general_dilated(values[None], weight, (1, 1, 1), ((0, 0), (0, 0)...  14.9 us
    ppermute x2, starting transfers between devices, padded_2(): after = lax.ppermute(first, axis, down)  10.1 us
    all_to_all x1, waiting for transfers between devices, body(): lax.all_to_all(outgoing, 'seq', split_axis=1, concat_axis=1, tiled=True)  9.04 us
    broadcast_in_dim x2, local copies, waits for them, and re-layouts, body(): doubled = jnp.repeat(jnp.repeat(extended, 2, axis=1)[:, 1:-1], 2, axis=2)  4.91 us
    sort x1, other arithmetic, body(): sending_order = jnp.argsort(own_numbers)  4.37 us
  transfers between devices with their start and end apart: 5, of which 2 were waited for; matrix products, arithmetic and copies ran while one was open for 10% of the time, Pallas kernels for 0%

commit v1 on v0

v1 whole, which is shorter than its diff:
```python
import jax
import jax.numpy as jnp
from jax import lax
from jax.experimental import pallas as pl
from jax.experimental.pallas import tpu as pltpu
from jax.sharding import PartitionSpec as P

LAT_CH = 16
MID_CH = 384
OUT_CH = 192
REQS = 8
FMAX = 3
ROWS_DEV = 4
W = 64
LANES = 128
HALO = 2
WIN_ROWS = ROWS_DEV + 2 * HALO
MID_ROWS = ROWS_DEV + 2
FX = FMAX * W
TILES = 3
BF16 = jnp.bfloat16
F32 = jnp.float32
I32 = jnp.int32
VMEM = pl.BlockSpec(memory_space=pltpu.VMEM)
SMEM = pl.BlockSpec(memory_space=pltpu.SMEM)
ANY = pl.BlockSpec(memory_space=pl.ANY)


def iota(shape, dim):
    return lax.broadcasted_iota(I32, shape, dim)


def dot(a, b, dims=((1,), (0,))):
    return lax.dot_general(a, b, (dims, ((), ())), preferred_element_type=F32)


NT = ((1,), (1,))


def cell_parts(numbers, assign_ref, devices):
    per_group = devices // REQS
    w_bits = W.bit_length() - 1
    height = ROWS_DEV * per_group
    h_bits = height.bit_length() - 1
    column = numbers & (W - 1)
    image_row = (numbers >> w_bits) & (height - 1)
    frames = numbers >> (w_bits + h_bits)
    request = jnp.zeros_like(frames)
    for r in range(1, REQS):
        request = request + (frames >= r * FMAX).astype(I32)
    frame = frames - request * FMAX
    group = jnp.zeros_like(frames)
    for g in range(1, REQS):
        group = jnp.where(request == assign_ref[g], g, group)
    place = group * per_group + image_row // ROWS_DEV
    target = (place - per_group // 2 + devices) & (devices - 1)
    return target, frame, image_row & (ROWS_DEV - 1), column


def earlier(length):
    return (iota((length, length), 0) < iota((length, length), 1)).astype(F32).astype(BF16)


def send_kernel(layout_ref, latents_ref, assign_ref, features_ref, out_ref, last_ref, first_ref, sems):
    devices, slots = layout_ref.shape
    per_peer = slots // devices
    me = lax.axis_index("seq")
    copies = [
        pltpu.make_async_copy(features_ref.at[:, ROWS_DEV - 1], last_ref, sems.at[0]),
        pltpu.make_async_copy(features_ref.at[:, 0], first_ref, sems.at[1]),
    ]
    for copy in copies:
        copy.start()
    base = pl.multiple_of(me // 8 * 8, 8)
    rows = layout_ref[pl.ds(base, 8), :]
    own = jnp.sum(jnp.where(iota(rows.shape, 0) == me - base, rows, 0), axis=0, keepdims=True)
    target = cell_parts(own, assign_ref, devices)[0]
    member = (iota((devices, slots), 0) == target).astype(F32)
    rank = dot(member.astype(BF16), earlier(slots))
    latents = latents_ref[...]
    out = jnp.zeros((devices, LANES), F32)
    for k in range(per_peer):
        picked = jnp.where(rank == float(k), member, 0.0).astype(BF16)
        cells = dot(picked, latents, NT).astype(BF16)
        spot = (iota((LAT_CH, LANES), 1) == iota((LAT_CH, LANES), 0) + k * LAT_CH).astype(F32)
        out = out + dot(cells, spot.astype(BF16))
    out_ref[:, 0:LANES] = pltpu.roll(out, 1, 0).astype(BF16)
    out_ref[:, LANES : 2 * LANES] = out.astype(BF16)
    out_ref[:, 2 * LANES : 3 * LANES] = pltpu.roll(out, devices - 1, 0).astype(BF16)
    for copy in copies:
        copy.wait()


def table_kernel(layout_ref, assign_ref, cache_ref, before_ref, after_ref, hot_ref, code_ref, cached_ref, spread):
    devices, slots = layout_ref.shape
    per_group = devices // REQS
    per_peer = slots // devices
    me = lax.axis_index("seq")
    place = (me + per_group // 2) & (devices - 1)
    position = place & (per_group - 1)
    target, frame, row, column = cell_parts(layout_ref[...], assign_ref, devices)
    order = earlier(slots)
    codes = jnp.zeros((devices, LANES), F32)
    fx = frame * W + column
    lane = iota((devices, LANES), 1)
    for j in range(TILES):
        tile = (me + j - 1 + devices) & (devices - 1)
        hit = target == tile
        rank = dot(hit.astype(F32).astype(BF16), order)
        code = ((row + ROWS_DEV * j) * 256 + fx).astype(F32)
        if j == 0:
            code = jnp.where(position == 0, 0.0, code)
        if j == TILES - 1:
            code = jnp.where(position == per_group - 1, 0.0, code)
        code = jnp.where(hit, code, 0.0)
        for k in range(per_peer):
            one = jnp.sum(jnp.where(rank == float(k), code, 0.0), axis=1, keepdims=True)
            codes = jnp.where(lane == j * per_peer + k, one, codes)
    code_ref[...] = codes
    across = jnp.transpose(codes).astype(I32) & 255
    for jk in range(TILES * per_peer):
        hot = (iota((FX, devices), 0) == across[jk : jk + 1, :]).astype(F32)
        hot_ref[:, jk * devices : (jk + 1) * devices] = hot.astype(BF16)
    width = W * LAT_CH
    keep = iota((W, width), 1) // LAT_CH == iota((W, width), 0)
    repeat = ((iota((width, LANES), 0) & (LAT_CH - 1)) == (iota((width, LANES), 1) & (LAT_CH - 1))).astype(F32).astype(BF16)
    lane = iota((W, LANES), 1) // LAT_CH
    for f in range(2):
        for y in range(WIN_ROWS):
            if y < HALO:
                line = before_ref[f, y + ROWS_DEV - HALO : y + ROWS_DEV - HALO + 1, :].astype(F32)
                line = jnp.where(position == 0, 0.0, line)
            elif y < HALO + ROWS_DEV:
                line = cache_ref[f, y - HALO : y - HALO + 1, :].astype(F32)
            else:
                line = after_ref[f, y - HALO - ROWS_DEV : y - HALO - ROWS_DEV + 1, :].astype(F32)
                line = jnp.where(position == per_group - 1, 0.0, line)
            spread[y * W : (y + 1) * W, :] = jnp.where(keep, line, 0.0).astype(BF16)
        wide = dot(spread[...], repeat)
        total = jnp.zeros((W, LANES), F32)
        for y in range(WIN_ROWS):
            total = jnp.where(lane == y, wide[y * W : (y + 1) * W, :], total)
        cached_ref[f * W : (f + 1) * W, :] = total.astype(BF16)


def weight_kernel(weight_ref, out_ref):
    taps = [[weight_ref[0, b, e].astype(F32) for e in range(3)] for b in range(3)]
    for a, i, rows in ((0, 0, (0,)), (0, 1, (1, 2)), (1, 0, (0, 1)), (1, 1, (2,))):
        line = [sum(taps[b][e] for b in rows[1:]) + taps[rows[0]][e] if len(rows) > 1 else taps[rows[0]][e] for e in range(3)]
        parts = (line[1] + line[2], line[0] + line[1], line[0], line[2])
        for g, part in enumerate(parts):
            out_ref[a, g * OUT_CH : (g + 1) * OUT_CH, i * MID_CH : (i + 1) * MID_CH] = part.astype(BF16)


def shifted(values, step, columns):
    if step == 1:
        return values
    rows = values.shape[0]
    x = iota(values.shape, 0) & (columns - 1)
    if step == 0:
        return jnp.where(x == 0, 0.0, pltpu.roll(values, 1, 0))
    return jnp.where(x == columns - 1, 0.0, pltpu.roll(values, rows - 1, 0))


def decode_kernel(
    incoming_ref,
    hot_ref,
    code_ref,
    cached_ref,
    assign_ref,
    counts_ref,
    first_weight_ref,
    first_bias_ref,
    gain_ref,
    second_bias_ref,
    features_ref,
    before_ref,
    after_ref,
    weight_ref,
    out_ref,
    latent_ref,
    next_ref,
    weight,
    second,
    padded,
    cells,
    window,
    decoded,
    sems,
    out_sems,
):
    devices = lax.axis_size("seq")
    per_group = devices // REQS
    me = lax.axis_index("seq")
    place = (me + per_group // 2) & (devices - 1)
    position = place & (per_group - 1)
    live = counts_ref[assign_ref[place // per_group]]
    copies = [
        pltpu.make_async_copy(features_ref, second.at[0:2, 1 : 1 + ROWS_DEV], sems.at[0]),
        pltpu.make_async_copy(before_ref, second.at[0:2, 0], sems.at[1]),
        pltpu.make_async_copy(after_ref, second.at[0:2, MID_ROWS - 1], sems.at[2]),
        pltpu.make_async_copy(weight_ref, weight, sems.at[3]),
    ]
    for copy in copies:
        copy.start()

    margin = (WIN_ROWS - 3) * LAT_CH
    for a in range(3):
        for e in range(3):
            padded[a * 3 + e, 0:margin, :] = jnp.zeros((margin, MID_CH), BF16)
            padded[a * 3 + e, margin + 3 * LAT_CH :, :] = jnp.zeros((margin, MID_CH), BF16)
            for b in range(3):
                padded[a * 3 + e, margin + b * LAT_CH : margin + (b + 1) * LAT_CH, :] = first_weight_ref[a, b, e]

    pairs = hot_ref.shape[1] // devices
    per_peer = pairs // TILES
    wide = per_peer * LANES
    source = iota((LANES, wide), 1)
    expand = (iota((LANES, wide), 0) == source // LANES * LAT_CH + (source & (LAT_CH - 1))).astype(F32).astype(BF16)
    codes = code_ref[...].astype(I32) >> 8
    lane = iota((devices, LANES), 1) // LAT_CH + HALO
    for j in range(TILES):
        spread = dot(incoming_ref[:, j * LANES : (j + 1) * LANES], expand)
        for k in range(per_peer):
            jk = j * per_peer + k
            part = jnp.where(lane == codes[:, jk : jk + 1], spread[:, k * LANES : (k + 1) * LANES], 0.0)
            cells[jk * devices : (jk + 1) * devices, :] = part.astype(BF16)
    arranged = dot(hot_ref[...], cells[...])
    frames = jnp.concatenate([cached_ref[...].astype(F32), arranged], axis=0)
    for e in range(3):
        window[e] = shifted(frames, e, W).astype(BF16)

    taps = jnp.concatenate([window[e, a * W : a * W + FX, :] for a in range(3) for e in range(3)], axis=1)
    for r in range(MID_ROWS):
        start = (MID_ROWS - 1 - r) * LAT_CH
        kernel = jnp.concatenate([padded[ae, start : start + LANES, :] for ae in range(9)], axis=0)
        pre = dot(taps, kernel) + first_bias_ref[...]
        inverse = lax.rsqrt(jnp.mean(pre * pre, axis=1, keepdims=True) + 1e-06)
        linear = pre * inverse * gain_ref[...]
        active = linear / (1.0 + jnp.exp(-linear))
        if r == 0:
            active = jnp.where(position == 0, 0.0, active)
        if r == MID_ROWS - 1:
            active = jnp.where(position == per_group - 1, 0.0, active)
        for t in range(FMAX):
            second[2 + t, r] = active[t * W : (t + 1) * W, :].astype(BF16)
    for copy in copies:
        copy.wait()

    @pl.when(position == 0)
    def _():
        second[0:2, 0] = jnp.zeros((2, W, MID_CH), BF16)

    @pl.when(position == per_group - 1)
    def _():
        second[0:2, MID_ROWS - 1] = jnp.zeros((2, W, MID_CH), BF16)

    ahead = pltpu.make_async_copy(second.at[pl.ds(live, 2), 1 : 1 + ROWS_DEV], next_ref, sems.at[0])
    ahead.start()

    width = W * LAT_CH
    kept = window[1, pl.ds(pl.multiple_of(live * W, W), 2 * W), :]
    own = iota((2 * W, width), 1) // LAT_CH == (iota((2 * W, width), 0) & (W - 1))
    for y in range(ROWS_DEV):
        pick = iota((LANES, width), 0) == (iota((LANES, width), 1) & (LAT_CH - 1)) + (HALO + y) * LAT_CH
        flat = jnp.where(own, dot(kept, pick.astype(F32).astype(BF16)), 0.0)
        for f in range(2):
            latent_ref[f, y : y + 1, :] = jnp.sum(flat[f * W : (f + 1) * W], axis=0, keepdims=True).astype(BF16)

    half = 2 * W
    pixels = ROWS_DEV * W
    diagonal = iota((OUT_CH, OUT_CH), 0) == iota((OUT_CH, OUT_CH), 1)
    bias = jnp.sum(jnp.where(diagonal, second_bias_ref[...], 0.0), axis=1, keepdims=True)
    column = iota((OUT_CH, pixels), 1) & (W - 1)
    at = iota((2 * half, 2 * half), 0)
    to = iota((2 * half, 2 * half), 1)
    source_row = (at & (half - 1)) // W
    weave = ((at & (W - 1)) * 2 + at // half + source_row * half == to).astype(F32).astype(BF16)
    sends = []
    for t in range(FMAX):
        for a in range(2):
            block = jnp.concatenate(
                [second[t + tau, a + i : a + i + ROWS_DEV].reshape(pixels, MID_CH) for tau in range(3) for i in range(2)],
                axis=1,
            )
            result = dot(weight[a], block, NT)
            left = pltpu.roll(result[2 * OUT_CH : 3 * OUT_CH], 1, 1)
            right = pltpu.roll(result[3 * OUT_CH : 4 * OUT_CH], pixels - 1, 1)
            even = result[0:OUT_CH] + jnp.where(column == 0, 0.0, left) + bias
            odd = result[OUT_CH : 2 * OUT_CH] + jnp.where(column == W - 1, 0.0, right) + bias
            even = jnp.where(t < live, even, 0.0).astype(BF16)
            odd = jnp.where(t < live, odd, 0.0).astype(BF16)
            for pair in range(ROWS_DEV // 2):
                lanes = slice(pair * half, (pair + 1) * half)
                woven = dot(jnp.concatenate([even[:, lanes], odd[:, lanes]], axis=1), weave).astype(BF16)
                for y in range(2):
                    decoded[t, 2 * (2 * pair + y) + a] = woven[:, y * half : (y + 1) * half]
        send = pltpu.make_async_copy(decoded.at[t], out_ref.at[t], out_sems.at[t])
        send.start()
        sends.append(send)
    for send in sends:
        send.wait()
    ahead.wait()


def body(
    latents,
    layout,
    assign,
    counts,
    latent_cache,
    feature_cache,
    first_weight,
    first_bias,
    norm_gain,
    second_weight,
    second_bias,
):
    devices = lax.axis_size("seq")
    slots = layout.shape[1]
    per_peer = slots // devices
    pairs = TILES * per_peer
    up = [(i, (i + 1) % devices) for i in range(devices)]
    down = [(j, i) for i, j in up]

    outgoing, last, first = pl.pallas_call(
        send_kernel,
        out_shape=(
            jax.ShapeDtypeStruct((devices, TILES * LANES), BF16),
            jax.ShapeDtypeStruct((2, W, MID_CH), BF16),
            jax.ShapeDtypeStruct((2, W, MID_CH), BF16),
        ),
        in_specs=[VMEM, VMEM, SMEM, ANY],
        out_specs=(VMEM, ANY, ANY),
        scratch_shapes=[pltpu.SemaphoreType.DMA((2,))],
        name="send",
    )(layout, latents, assign, feature_cache)
    latent_before = lax.ppermute(latent_cache, "seq", up)
    latent_after = lax.ppermute(latent_cache, "seq", down)
    feature_before = lax.ppermute(last, "seq", up)
    feature_after = lax.ppermute(first, "seq", down)
    incoming = lax.all_to_all(
        outgoing.reshape(devices, 1, TILES * LANES), "seq", split_axis=0, concat_axis=0, tiled=True
    ).reshape(devices, TILES * LANES)

    hot, codes, cached = pl.pallas_call(
        table_kernel,
        out_shape=(
            jax.ShapeDtypeStruct((FX, pairs * devices), BF16),
            jax.ShapeDtypeStruct((devices, LANES), F32),
            jax.ShapeDtypeStruct((2 * W, LANES), BF16),
        ),
        in_specs=[VMEM, SMEM, VMEM, VMEM, VMEM],
        out_specs=(VMEM, VMEM, VMEM),
        scratch_shapes=[pltpu.VMEM((WIN_ROWS * W, W * LAT_CH), BF16)],
        name="table",
    )(layout, assign, latent_cache, latent_before, latent_after)

    combined = pl.pallas_call(
        weight_kernel,
        grid=(3,),
        out_shape=jax.ShapeDtypeStruct((2, 4 * OUT_CH, 6 * MID_CH), BF16),
        in_specs=[pl.BlockSpec((1, 3, 3, OUT_CH, MID_CH), lambda t: (t, 0, 0, 0, 0))],
        out_specs=pl.BlockSpec((2, 4 * OUT_CH, 2 * MID_CH), lambda t: (0, 0, t)),
        name="combine",
    )(jnp.swapaxes(second_weight, 3, 4))

    decoded, latent_next, feature_next = pl.pallas_call(
        decode_kernel,
        out_shape=(
            jax.ShapeDtypeStruct((FMAX, 2 * ROWS_DEV, OUT_CH, 2 * W), BF16),
            jax.ShapeDtypeStruct((2, ROWS_DEV, W * LAT_CH), BF16),
            jax.ShapeDtypeStruct((2, ROWS_DEV, W, MID_CH), BF16),
        ),
        in_specs=[VMEM] * 4 + [SMEM] * 2 + [VMEM] * 4 + [ANY] * 4,
        out_specs=(ANY, VMEM, ANY),
        scratch_shapes=[
            pltpu.VMEM((2, 4 * OUT_CH, 6 * MID_CH), BF16),
            pltpu.VMEM((5, MID_ROWS, W, MID_CH), BF16),
            pltpu.VMEM((9, (2 * WIN_ROWS - 3) * LAT_CH, MID_CH), BF16),
            pltpu.VMEM((pairs * devices, LANES), BF16),
            pltpu.VMEM((3, 5 * W, LANES), BF16),
            pltpu.VMEM((FMAX, 2 * ROWS_DEV, OUT_CH, 2 * W), BF16),
            pltpu.SemaphoreType.DMA((4,)),
            pltpu.SemaphoreType.DMA((FMAX,)),
        ],
        name="decode",
    )(
        incoming,
        hot,
        codes,
        cached,
        assign,
        counts,
        first_weight,
        first_bias.reshape(1, MID_CH),
        norm_gain.reshape(1, MID_CH),
        second_bias.reshape(1, OUT_CH),
        feature_cache,
        feature_before,
        feature_after,
        combined,
    )
    return (jnp.swapaxes(decoded, 2, 3), latent_next, feature_next)


def solution(mesh):
    return jax.shard_map(
        body,
        mesh=mesh,
        in_specs=(
            P(None, ("rep", "seq")),
            P("rep", None),
            P("rep"),
            P("rep"),
            P(None, ("rep", "seq"), None),
            P(None, ("rep", "seq"), None, None),
            P(),
            P(),
            P(),
            P(),
            P(),
        ),
        out_specs=(
            P(None, ("rep", "seq"), None, None),
            P(None, ("rep", "seq"), None),
            P(None, ("rep", "seq"), None, None),
        ),
        check_vma=False,
    )
```

time: 164 us -> 89.9 us (0.55)
  local copies, waits for them, and re-layouts: 52.7 us -> 6.58 us
  Pallas kernels: 0 us -> 38.1 us
  matrix products: 20.5 us -> 0 us
  other arithmetic: 20.9 us -> 1.56 us
  between operations: 16 us -> 0.85 us
  waiting for transfers between devices: 9.77 us -> 0.01 us
    pallas_call x0 -> x4, Pallas kernels: none -> 38.1 us  [the longest x1 18.5 us: body(): pl.pallas_call(decode_kernel, out_shape=(jax.ShapeDtypeStruct((FMAX, 2 *...]
    conv_general_dilated x2 -> x0, matrix products: 20.5 us -> none  [causal_conv(): lax.conv_general_dilated(values[None], weight, (1, 1, 1), ((0, 0), (0, 0)...]
    another operation x4 -> x0, local copies, waits for them, and re-layouts: 19.6 us -> none  [the longest x2 18.3 us: causal_conv(): values[None]]
    conv_general_dilated x7 -> x0, local copies, waits for them, and re-layouts: 14.9 us -> none  [causal_conv(): lax.conv_general_dilated(values[None], weight, (1, 1, 1), ((0, 0), (0, 0)...]
    all_to_all x1, waiting for transfers between devices: 9.04 us -> 0.01 us  [body(): lax.all_to_all(outgoing.reshape(devices, 1, TILES * LANES), 'seq', split_...]
    sort x2 -> x0, other arithmetic: 8.74 us -> none  [the longest x1 4.37 us: body(): sending_order = jnp.argsort(own_numbers)]
    broadcast_in_dim x2 -> x0, local copies, waits for them, and re-layouts: 4.91 us -> none  [body(): doubled = jnp.repeat(jnp.repeat(extended, 2, axis=1)[:, 1:-1], 2, axis=2)]
    select_n x7 -> x0, other arithmetic: 4.29 us -> none  [the longest x2 2.16 us: keep_rows(): jnp.where(inside[None, :, None, None], values, jnp.zeros((), values.dtype))]
  transfers between devices with their start and end apart: 5 -> 5, of which waited for: 2 -> 0; matrix products, arithmetic and copies ran while one was open for 10% -> 4% of each run, Pallas kernels for 0% -> 12%
where the time goes in v1:
time: 89.9 us; the launch traced here: 89.5 us
  starting transfers between devices  42.4 us (47%)
  Pallas kernels  38.1 us (42%)
  local copies, waits for them, and re-layouts  6.58 us (7%)
  other arithmetic  1.56 us (2%)
    all_to_all x1, starting transfers between devices, body(): lax.all_to_all(outgoing.reshape(devices, 1, TILES * LANES), 'seq', split_...  32.2 us
    pallas_call x1, Pallas kernels, body(): pl.pallas_call(decode_kernel, out_shape=(jax.ShapeDtypeStruct((FMAX, 2 *...  18.5 us
    pallas_call x1, Pallas kernels, body(): pl.pallas_call(send_kernel, out_shape=(jax.ShapeDtypeStruct((devices, TIL...  8.73 us
    pallas_call x1, Pallas kernels, body(): pl.pallas_call(weight_kernel, grid=(3,), out_shape=jax.ShapeDtypeStruct((...  6.1 us
    ppermute x1, starting transfers between devices, body(): latent_after = lax.ppermute(latent_cache, 'seq', down)  5.06 us
    ppermute x1, starting transfers between devices, body(): feature_after = lax.ppermute(first, 'seq', down)  5.04 us
    pallas_call x1, Pallas kernels, body(): pl.pallas_call(table_kernel, out_shape=(jax.ShapeDtypeStruct((FX, pairs *...  4.78 us
    unnamed x11, local copies, waits for them, and re-layouts  3.53 us
  transfers between devices with their start and end apart: 5, of which 0 were waited for; matrix products, arithmetic and copies ran while one was open for 4% of the time, Pallas kernels for 12%

profile of v1, /device:TPU:40, one launch (start us, length us, event | category | flops | bytes accessed | tf_op | source)
XLA Modules:
  0.0 89.5 jit_solution(4717930504396320822)
XLA Ops:
  0.6 8.7 %send.1 = (bf16[128,384]{1,0:T(8,128)(2,1)}, bf16[2,64,384]{2,1,0:T(8,128)(2,1)}, bf16[2,64,384]{2,1,0:T(8,128)(2,1)}) custom-call(s32[128,768]{1,0:T(8,128)} %layout_ref.3, bf16[16,768]{1,0:T(8,128)(2,1)} %latents_ref.1, s32[8]{0:T(128)} %assign_ref.5, bf16[2,4,64,384]{3,2,1,0:T(8,128)(2,1)} %features_ref.3), custom_call_target="tpu_custom_call" | custom-call | tf_op jit(solution)/shard_map/send/pallas_call | solution.py:326
  9.4 0.5 broadcast
  9.9 1.6 %reduce = bf16[128,384]{1,0:T(8,128)(2,1)S(1)} reduce(bf16[128,1,384]{2,0,1:T(8,128)(2,1)} %bitcast.9, bf16[]{:T(256)} %broadcast), dimensions={1}, to_apply=%copy.15.reduce_sub_computation | reduce | bytes 196610 | tf_op jit(solution)/shard_map/reshape | solution.py:343
  11.4 0.8 reshape.26
  12.2 32.2 %all-to-all-start = ((bf16[128,2,192]{2,1,0:T(2,128)(2,1)}), bf16[128,2,192]{2,1,0:T(2,128)(2,1)S(1)}, u32[]{:S(2)}, u32[]{:S(2)}) async-start(bf16[128,2,192]{2,1,0:T(2,128)(2,1)} %reshape.26), calls=%async_computation | async-start | bytes 262144 | tf_op jit(solution)/shard_map/all_to_all | solution.py:342
  44.4 0.1 collective-permute-start.2
  44.5 5.0 %collective-permute-start.3 = (bf16[2,64,384]{2,1,0:T(8,128)(2,1)}, bf16[2,64,384]{2,1,0:T(8,128)(2,1)S(1)}, u32[]{:S(2)}, u32[]{:S(2)}) collective-permute-start(bf16[2,64,384]{2,1,0:T(8,128)(2,1)} %get-tuple-element.17), channel_id=1, source_target_pairs={{1,0},{2,1},{3,2},{4,3},{5,4},{6,5},{7,6},{8,7},{9,8},{10,9},{11,1... | collective-permute-start | bytes 294920 | tf_op jit(solution)/shard_map/ppermute | solution.py:341
  49.6 0.0 collective-permute-start
  49.6 5.1 %collective-permute-start.1 = (bf16[2,4,1024]{2,1,0:T(4,128)(2,1)}, bf16[2,4,1024]{2,1,0:T(4,128)(2,1)S(1)}, u32[]{:S(2)}, u32[]{:S(2)}) collective-permute-start(bf16[2,4,1024]{2,1,0:T(4,128)(2,1)} %cache_ref.1), channel_id=1, source_target_pairs={{1,0},{2,1},{3,2},{4,3},{5,4},{6,5},{7,6},{8,7},{9,8},{10,9},{11,1... | collective-permute-start | bytes 49160 | tf_op jit(solution)/shard_map/ppermute | solution.py:339
  54.6 1.3 %reshape.23.first_bias_ref = f32[1,384]{1,0:T(1,128)} reshape(f32[384]{0:T(512)} %param.18) | data formatting | bytes 3072 | tf_op jit(solution)/shard_map/reshape | solution.py:396
  55.9 1.3 %reshape.24.gain_ref = f32[1,384]{1,0:T(1,128)} reshape(f32[384]{0:T(512)} %param.19) | data formatting | bytes 3072 | tf_op jit(solution)/shard_map/reshape | solution.py:397
  57.2 6.1 %combine.1.weight_ref = bf16[2,768,2304]{2,1,0:T(8,128)(2,1)} custom-call(bf16[3,3,3,192,384]{4,3,2,1,0:T(8,128)(2,1)} %bitcast.7), custom_call_target="tpu_custom_call" | custom-call | tf_op jit(solution)/shard_map/combine/pallas_call | solution.py:359
  63.3 0.0 collective-permute-done.before_ref
  63.3 0.0 copy-start.2
  63.3 0.0 collective-permute-done.1.after_ref
  63.3 0.6 copy-done.2
  63.9 0.0 copy-start.3
  63.9 0.6 copy-done.3
  64.5 4.8 %table.1 = (bf16[192,2304]{1,0:T(8,128)(2,1)}, f32[128,128]{1,0:T(8,128)}, bf16[128,128]{1,0:T(8,128)(2,1)}) custom-call(s32[128,768]{1,0:T(8,128)} %layout_ref.3, s32[8]{0:T(128)} %assign_ref.5, bf16[2,4,1024]{2,1,0:T(4,128)(2,1)} %cache_ref.1, bf16[2,4,1024]{2,1,0:T(4,128)(2,1)} %copy-done.2, bf16[2,4,1024]{2,1,0:T(4,128)(2,1)} %copy-done.3), custom_call_target="tpu_custom_call" | custom-call | tf_op jit(solution)/shard_map/table/pallas_call | solution.py:346
  69.3 0.0 all-to-all-done
  69.3 0.2 reshape.27
  69.4 0.7 copy.18
  70.1 0.0 collective-permute-done.2.before_ref
  70.1 0.0 copy-start
  70.1 0.0 collective-permute-done.3.after_ref
  70.1 0.0 copy-start.1
  70.1 0.6 copy-done
  70.8 0.1 copy-done.1
  70.8 18.5 %decode.1 = (bf16[3,8,192,128]{3,2,1,0:T(8,128)(2,1)}, bf16[2,4,1024]{2,1,0:T(4,128)(2,1)}, bf16[2,4,64,384]{3,2,1,0:T(8,128)(2,1)}) custom-call(bf16[128,384]{1,0:T(8,128)(2,1)} %bitcast.8, bf16[192,2304]{1,0:T(8,128)(2,1)} %get-tuple-element.13.hot_ref, f32[128,128]{1,0:T(8,128)} %get-tuple-element.14.code_ref, ...), custom_call_target="tpu_custom_call" | custom-call | tf_op jit(solution)/shard_map/decode/pallas_call | solution.py:368
Async XLA Ops:
  12.2 57.0 %all-to-all-start = ((bf16[128,2,192]{2,1,0:T(2,128)(2,1)}), bf16[128,2,192]{2,1,0:T(2,128)(2,1)S(1)}, u32[]{:S(2)}, u32[]{:S(2)}) async-start(bf16[128,2,192]{2,1,0:T(2,128)(2,1)} %reshape.26), calls=%async_computation | async-start | bytes 262144 | tf_op jit(solution)/shard_map/all_to_all | solution.py:342
  44.4 25.7 %collective-permute-start.2 = (bf16[2,64,384]{2,1,0:T(8,128)(2,1)}, bf16[2,64,384]{2,1,0:T(8,128)(2,1)S(1)}, u32[]{:S(2)}, u32[]{:S(2)}) collective-permute-start(bf16[2,64,384]{2,1,0:T(8,128)(2,1)} %get-tuple-element.16), channel_id=1, source_target_pairs={{0,1},{1,2},{2,3},{3,4},{4,5},{5,6},{6,7},{7,8},{8,9},{9,10},{10,1... | collective-permute-start | bytes 294920 | tf_op jit(solution)/shard_map/ppermute | solution.py:340
  44.5 25.6 %collective-permute-start.3 = (bf16[2,64,384]{2,1,0:T(8,128)(2,1)}, bf16[2,64,384]{2,1,0:T(8,128)(2,1)S(1)}, u32[]{:S(2)}, u32[]{:S(2)}) collective-permute-start(bf16[2,64,384]{2,1,0:T(8,128)(2,1)} %get-tuple-element.17), channel_id=1, source_target_pairs={{1,0},{2,1},{3,2},{4,3},{5,4},{6,5},{7,6},{8,7},{9,8},{10,9},{11,1... | collective-permute-start | bytes 294920 | tf_op jit(solution)/shard_map/ppermute | solution.py:341
  49.6 13.7 %collective-permute-start = (bf16[2,4,1024]{2,1,0:T(4,128)(2,1)}, bf16[2,4,1024]{2,1,0:T(4,128)(2,1)S(1)}, u32[]{:S(2)}, u32[]{:S(2)}) collective-permute-start(bf16[2,4,1024]{2,1,0:T(4,128)(2,1)} %cache_ref.1), channel_id=1, source_target_pairs={{0,1},{1,2},{2,3},{3,4},{4,5},{5,6},{6,7},{7,8},{8,9},{9,10},{10,1... | collective-permute-start | bytes 49160 | tf_op jit(solution)/shard_map/ppermute | solution.py:338
  49.6 13.7 %collective-permute-start.1 = (bf16[2,4,1024]{2,1,0:T(4,128)(2,1)}, bf16[2,4,1024]{2,1,0:T(4,128)(2,1)S(1)}, u32[]{:S(2)}, u32[]{:S(2)}) collective-permute-start(bf16[2,4,1024]{2,1,0:T(4,128)(2,1)} %cache_ref.1), channel_id=1, source_target_pairs={{1,0},{2,1},{3,2},{4,3},{5,4},{6,5},{7,6},{8,7},{9,8},{10,9},{11,1... | collective-permute-start | bytes 49160 | tf_op jit(solution)/shard_map/ppermute | solution.py:339
  63.3 0.6 copy-start.2
  63.9 0.6 copy-start.3
  70.1 0.7 copy-start
  70.1 0.7 copy-start.1

commit v2 on v1

--- a/solution.py
+++ b/solution.py
@@ -18,6 +18,8 @@
 MID_ROWS = ROWS_DEV + 2
 FX = FMAX * W
 TILES = 3
+SLOTS = 4
+PIECES = ((0, 384), (384, 768), (768, 1024))
 BF16 = jnp.bfloat16
 F32 = jnp.float32
 I32 = jnp.int32
@@ -61,22 +63,32 @@
     return (iota((length, length), 0) < iota((length, length), 1)).astype(F32).astype(BF16)
 
 
-def send_kernel(layout_ref, latents_ref, assign_ref, features_ref, out_ref, last_ref, first_ref, sems):
+def send_kernel(layout_ref, latents_ref, assign_ref, features_ref, cache_ref, out_ref, last_ref, first_ref, rows, wide, sems):
     devices, slots = layout_ref.shape
     per_peer = slots // devices
     me = lax.axis_index("seq")
+    base = pl.multiple_of(me // 8 * 8, 8)
     copies = [
-        pltpu.make_async_copy(features_ref.at[:, ROWS_DEV - 1], last_ref, sems.at[0]),
-        pltpu.make_async_copy(features_ref.at[:, 0], first_ref, sems.at[1]),
+        pltpu.make_async_copy(layout_ref.at[pl.ds(base, 8)], rows, sems.at[0]),
+        pltpu.make_async_copy(features_ref.at[:, ROWS_DEV - 1], last_ref.at[:, 0:W], sems.at[1]),
+        pltpu.make_async_copy(features_ref.at[:, 0], first_ref.at[:, 0:W], sems.at[2]),
     ]
     for copy in copies:
         copy.start()
-    base = pl.multiple_of(me // 8 * 8, 8)
-    rows = layout_ref[pl.ds(base, 8), :]
-    own = jnp.sum(jnp.where(iota(rows.shape, 0) == me - base, rows, 0), axis=0, keepdims=True)
+    for ref, top in ((last_ref, ROWS_DEV - HALO), (first_ref, 0)):
+        for f in range(2):
+            ref[f, W:, :] = jnp.zeros((ref.shape[1] - W, MID_CH), BF16)
+            for y in range(HALO):
+                for p, (low, high) in enumerate(PIECES):
+                    at = W + y * len(PIECES) + p
+                    ref[f, at : at + 1, 0 : high - low] = cache_ref[f, top + y : top + y + 1, low:high]
+    order = earlier(slots)
+    wide[...] = jnp.zeros(wide.shape, F32)
+    copies[0].wait()
+    own = jnp.sum(jnp.where(iota(rows.shape, 0) == me - base, rows[...], 0), axis=0, keepdims=True)
     target = cell_parts(own, assign_ref, devices)[0]
     member = (iota((devices, slots), 0) == target).astype(F32)
-    rank = dot(member.astype(BF16), earlier(slots))
+    rank = dot(member.astype(BF16), order)
     latents = latents_ref[...]
     out = jnp.zeros((devices, LANES), F32)
     for k in range(per_peer):
@@ -84,11 +96,18 @@
         cells = dot(picked, latents, NT).astype(BF16)
         spot = (iota((LAT_CH, LANES), 1) == iota((LAT_CH, LANES), 0) + k * LAT_CH).astype(F32)
         out = out + dot(cells, spot.astype(BF16))
-    out_ref[:, 0:LANES] = pltpu.roll(out, 1, 0).astype(BF16)
-    out_ref[:, LANES : 2 * LANES] = out.astype(BF16)
-    out_ref[:, 2 * LANES : 3 * LANES] = pltpu.roll(out, devices - 1, 0).astype(BF16)
-    for copy in copies:
-        copy.wait()
+    wide[pl.ds(0, devices, stride=SLOTS), :] = pltpu.roll(out, 1, 0)
+    wide[pl.ds(1, devices, stride=SLOTS), :] = out
+    wide[pl.ds(2, devices, stride=SLOTS), :] = pltpu.roll(out, devices - 1, 0)
+    out_ref[...] = wide[...].astype(BF16)
+    copies[1].wait()
+    copies[2].wait()
+
+
+def halo_line(ref, f, y):
+    start = W + y * len(PIECES)
+    parts = [ref[f, start + p : start + p + 1, 0 : high - low].astype(F32) for p, (low, high) in enumerate(PIECES)]
+    return jnp.concatenate(parts, axis=1)
 
 
 def table_kernel(layout_ref, assign_ref, cache_ref, before_ref, after_ref, hot_ref, code_ref, cached_ref, spread):
@@ -128,12 +147,12 @@
     for f in range(2):
         for y in range(WIN_ROWS):
             if y < HALO:
-                line = before_ref[f, y + ROWS_DEV - HALO : y + ROWS_DEV - HALO + 1, :].astype(F32)
+                line = halo_line(before_ref, f, y)
                 line = jnp.where(position == 0, 0.0, line)
             elif y < HALO + ROWS_DEV:
                 line = cache_ref[f, y - HALO : y - HALO + 1, :].astype(F32)
             else:
-                line = after_ref[f, y - HALO - ROWS_DEV : y - HALO - ROWS_DEV + 1, :].astype(F32)
+                line = halo_line(after_ref, f, y - HALO - ROWS_DEV)
                 line = jnp.where(position == per_group - 1, 0.0, line)
             spread[y * W : (y + 1) * W, :] = jnp.where(keep, line, 0.0).astype(BF16)
         wide = dot(spread[...], repeat)
@@ -185,6 +204,8 @@
     padded,
     cells,
     window,
+    received,
+    halves,
     decoded,
     sems,
     out_sems,
@@ -197,8 +218,8 @@
     live = counts_ref[assign_ref[place // per_group]]
     copies = [
         pltpu.make_async_copy(features_ref, second.at[0:2, 1 : 1 + ROWS_DEV], sems.at[0]),
-        pltpu.make_async_copy(before_ref, second.at[0:2, 0], sems.at[1]),
-        pltpu.make_async_copy(after_ref, second.at[0:2, MID_ROWS - 1], sems.at[2]),
+        pltpu.make_async_copy(before_ref.at[:, 0:W], second.at[0:2, 0], sems.at[1]),
+        pltpu.make_async_copy(after_ref.at[:, 0:W], second.at[0:2, MID_ROWS - 1], sems.at[2]),
         pltpu.make_async_copy(weight_ref, weight, sems.at[3]),
     ]
     for copy in copies:
@@ -219,8 +240,9 @@
     expand = (iota((LANES, wide), 0) == source // LANES * LAT_CH + (source & (LAT_CH - 1))).astype(F32).astype(BF16)
     codes = code_ref[...].astype(I32) >> 8
     lane = iota((devices, LANES), 1) // LAT_CH + HALO
+    received[...] = incoming_ref[...].astype(F32)
     for j in range(TILES):
-        spread = dot(incoming_ref[:, j * LANES : (j + 1) * LANES], expand)
+        spread = dot(received[pl.ds(j, devices, stride=SLOTS), :].astype(BF16), expand)
         for k in range(per_peer):
             jk = j * per_peer + k
             part = jnp.where(lane == codes[:, jk : jk + 1], spread[:, k * LANES : (k + 1) * LANES], 0.0)
@@ -234,9 +256,9 @@
     for r in range(MID_ROWS):
         start = (MID_ROWS - 1 - r) * LAT_CH
         kernel = jnp.concatenate([padded[ae, start : start + LANES, :] for ae in range(9)], axis=0)
-        pre = dot(taps, kernel) + first_bias_ref[...]
+        pre = dot(taps, kernel) + first_bias_ref[...][None, :]
         inverse = lax.rsqrt(jnp.mean(pre * pre, axis=1, keepdims=True) + 1e-06)
-        linear = pre * inverse * gain_ref[...]
+        linear = pre * inverse * gain_ref[...][None, :]
         active = linear / (1.0 + jnp.exp(-linear))
         if r == 0:
             active = jnp.where(position == 0, 0.0, active)
@@ -270,13 +292,8 @@
     half = 2 * W
     pixels = ROWS_DEV * W
     diagonal = iota((OUT_CH, OUT_CH), 0) == iota((OUT_CH, OUT_CH), 1)
-    bias = jnp.sum(jnp.where(diagonal, second_bias_ref[...], 0.0), axis=1, keepdims=True)
+    bias = jnp.sum(jnp.where(diagonal, second_bias_ref[...][None, :], 0.0), axis=1, keepdims=True)
     column = iota((OUT_CH, pixels), 1) & (W - 1)
-    at = iota((2 * half, 2 * half), 0)
-    to = iota((2 * half, 2 * half), 1)
-    source_row = (at & (half - 1)) // W
-    weave = ((at & (W - 1)) * 2 + at // half + source_row * half == to).astype(F32).astype(BF16)
-    sends = []
     for t in range(FMAX):
         for a in range(2):
             block = jnp.concatenate(
@@ -292,14 +309,25 @@
             odd = jnp.where(t < live, odd, 0.0).astype(BF16)
             for pair in range(ROWS_DEV // 2):
                 lanes = slice(pair * half, (pair + 1) * half)
-                woven = dot(jnp.concatenate([even[:, lanes], odd[:, lanes]], axis=1), weave).astype(BF16)
+                at = (pair * 2 + a) * OUT_CH
+                halves[t, at : at + OUT_CH, 0:half] = even[:, lanes]
+                halves[t, at : at + OUT_CH, half : 2 * half] = odd[:, lanes]
+
+    @pl.loop(0, FMAX)
+    def _(t):
+        at = iota((2 * half, 2 * half), 0)
+        to = iota((2 * half, 2 * half), 1)
+        source_row = (at & (half - 1)) // W
+        weave = ((at & (W - 1)) * 2 + at // half + source_row * half == to).astype(F32).astype(BF16)
+        woven = dot(halves[t], weave).astype(BF16)
+        for pair in range(ROWS_DEV // 2):
+            for a in range(2):
+                start = (pair * 2 + a) * OUT_CH
                 for y in range(2):
-                    decoded[t, 2 * (2 * pair + y) + a] = woven[:, y * half : (y + 1) * half]
-        send = pltpu.make_async_copy(decoded.at[t], out_ref.at[t], out_sems.at[t])
-        send.start()
-        sends.append(send)
-    for send in sends:
-        send.wait()
+                    decoded[t, 2 * (2 * pair + y) + a] = woven[start : start + OUT_CH, y * half : (y + 1) * half]
+        pltpu.make_async_copy(decoded.at[t], out_ref.at[t], out_sems.at[0]).start()
+
+    pltpu.make_async_copy(decoded, out_ref, out_sems.at[0]).wait()
     ahead.wait()
 
 
@@ -323,25 +351,24 @@
     up = [(i, (i + 1) % devices) for i in range(devices)]
     down = [(j, i) for i, j in up]
 
+    edge = jax.ShapeDtypeStruct((2, W + 8, MID_CH), BF16)
     outgoing, last, first = pl.pallas_call(
         send_kernel,
-        out_shape=(
-            jax.ShapeDtypeStruct((devices, TILES * LANES), BF16),
-            jax.ShapeDtypeStruct((2, W, MID_CH), BF16),
-            jax.ShapeDtypeStruct((2, W, MID_CH), BF16),
-        ),
-        in_specs=[VMEM, VMEM, SMEM, ANY],
-        out_specs=(VMEM, ANY, ANY),
-        scratch_shapes=[pltpu.SemaphoreType.DMA((2,))],
+        out_shape=(jax.ShapeDtypeStruct((devices * SLOTS, LANES), BF16), edge, edge),
+        in_specs=[ANY, VMEM, SMEM, ANY, VMEM],
+        out_specs=(VMEM, VMEM, VMEM),
+        scratch_shapes=[
+            pltpu.VMEM((8, slots), I32),
+            pltpu.VMEM((devices * SLOTS, LANES), F32),
+            pltpu.SemaphoreType.DMA((3,)),
+        ],
         name="send",
-    )(layout, latents, assign, feature_cache)
-    latent_before = lax.ppermute(latent_cache, "seq", up)
-    latent_after = lax.ppermute(latent_cache, "seq", down)
-    feature_before = lax.ppermute(last, "seq", up)
-    feature_after = lax.ppermute(first, "seq", down)
+    )(layout, latents, assign, feature_cache, latent_cache)
+    before = lax.ppermute(last, "seq", up)
+    after = lax.ppermute(first, "seq", down)
     incoming = lax.all_to_all(
-        outgoing.reshape(devices, 1, TILES * LANES), "seq", split_axis=0, concat_axis=0, tiled=True
-    ).reshape(devices, TILES * LANES)
+        outgoing.reshape(devices, SLOTS, LANES), "seq", split_axis=0, concat_axis=0, tiled=True
+    ).reshape(devices * SLOTS, LANES)
 
     hot, codes, cached = pl.pallas_call(
         table_kernel,
@@ -354,7 +381,7 @@
         out_specs=(VMEM, VMEM, VMEM),
         scratch_shapes=[pltpu.VMEM((WIN_ROWS * W, W * LAT_CH), BF16)],
         name="table",
-    )(layout, assign, latent_cache, latent_before, latent_after)
+    )(layout, assign, latent_cache, before, after)
 
     combined = pl.pallas_call(
         weight_kernel,
@@ -380,9 +407,11 @@
             pltpu.VMEM((9, (2 * WIN_ROWS - 3) * LAT_CH, MID_CH), BF16),
             pltpu.VMEM((pairs * devices, LANES), BF16),
             pltpu.VMEM((3, 5 * W, LANES), BF16),
+            pltpu.VMEM((devices * SLOTS, LANES), F32),
+            pltpu.VMEM((FMAX, ROWS_DEV * OUT_CH, 4 * W), BF16),
             pltpu.VMEM((FMAX, 2 * ROWS_DEV, OUT_CH, 2 * W), BF16),
             pltpu.SemaphoreType.DMA((4,)),
-            pltpu.SemaphoreType.DMA((FMAX,)),
+            pltpu.SemaphoreType.DMA((1,)),
         ],
         name="decode",
     )(
@@ -393,12 +422,12 @@
         assign,
         counts,
         first_weight,
-        first_bias.reshape(1, MID_CH),
-        norm_gain.reshape(1, MID_CH),
-        second_bias.reshape(1, OUT_CH),
+        first_bias,
+        norm_gain,
+        second_bias,
         feature_cache,
-        feature_before,
-        feature_after,
+        before,
+        after,
         combined,
     )
     return (jnp.swapaxes(decoded, 2, 3), latent_next, feature_next)

time: 89.9 us -> 67.9 us (0.76)
  Pallas kernels: 38.1 us -> 27.4 us
  starting transfers between devices: 42.4 us -> 37.3 us
  local copies, waits for them, and re-layouts: 6.58 us -> 1.96 us
  other arithmetic: 1.56 us -> 0 us
    pallas_call x1, Pallas kernels: 18.5 us -> 13 us  [body(): pl.pallas_call(decode_kernel, out_shape=(jax.ShapeDtypeStruct((FMAX, 2 *...]
    pallas_call x1, Pallas kernels: 8.73 us -> 3.5 us  [body(): pl.pallas_call(send_kernel, out_shape=(jax.ShapeDtypeStruct((devices * SL...]
    ppermute x4 -> x2, starting transfers between devices: 10.2 us -> 5.17 us  [the longest x1 5.04 us: body(): after = lax.ppermute(first, 'seq', down)]
    reshape x3 -> x0, local copies, waits for them, and re-layouts: 3.04 us -> none  [the longest x1 1.27 us: body(): norm_gain.reshape(1, MID_CH)]
    unnamed x11 -> x6, local copies, waits for them, and re-layouts: 3.53 us -> 1.96 us
    reshape x1 -> x0, other arithmetic: 1.56 us -> none  [body(): outgoing.reshape(devices, 1, TILES * LANES)]
  transfers between devices with their start and end apart: 5 -> 3, of which waited for: 0 -> 0; matrix products, arithmetic and copies ran while one was open for 4% -> 0% of each run, Pallas kernels for 12% -> 16%
where the time goes in v2:
time: 67.9 us; the launch traced here: 67.6 us
  starting transfers between devices  37.3 us (55%)
  Pallas kernels  27.4 us (40%)
  local copies, waits for them, and re-layouts  1.96 us (3%)
  between operations  0.83 us (1%)
    all_to_all x1, starting transfers between devices, body(): lax.all_to_all(outgoing.reshape(devices, SLOTS, LANES), 'seq', split_axis...  32.2 us
    pallas_call x1, Pallas kernels, body(): pl.pallas_call(decode_kernel, out_shape=(jax.ShapeDtypeStruct((FMAX, 2 *...  13 us
    pallas_call x1, Pallas kernels, body(): pl.pallas_call(weight_kernel, grid=(3,), out_shape=jax.ShapeDtypeStruct((...  6.1 us
    ppermute x1, starting transfers between devices, body(): after = lax.ppermute(first, 'seq', down)  5.04 us
    pallas_call x1, Pallas kernels, body(): pl.pallas_call(table_kernel, out_shape=(jax.ShapeDtypeStruct((FX, pairs *...  4.83 us
    pallas_call x1, Pallas kernels, body(): pl.pallas_call(send_kernel, out_shape=(jax.ShapeDtypeStruct((devices * SL...  3.5 us
    unnamed x6, local copies, waits for them, and re-layouts  1.96 us
  transfers between devices with their start and end apart: 3, of which 0 were waited for; matrix products, arithmetic and copies ran while one was open for 0% of the time, Pallas kernels for 16%

profile of v2, /device:TPU:40, one launch (start us, length us, event | category | flops | bytes accessed | tf_op | source)
XLA Modules:
  0.0 67.6 jit_solution(6810525721300975875)
XLA Ops:
  0.6 3.5 %send.1 = (bf16[512,128]{1,0:T(8,128)(2,1)}, bf16[2,72,384]{2,1,0:T(8,128)(2,1)}, bf16[2,72,384]{2,1,0:T(8,128)(2,1)}) custom-call(s32[128,768]{1,0:T(8,128)} %layout_ref.3, bf16[16,768]{1,0:T(8,128)(2,1)} %latents_ref.1, s32[8]{0:T(128)} %assign_ref.5, bf16[2,4,64,384]{3,2,1,0:T(8,128)(2,1)} %features_ref.3, bf16[2,4,1024]{2,1,0:T(4,128)(2,1)} %cache_ref.3), custom_call_target="tpu_custom_call" | custom-call | tf_op jit(solution)/shard_map/send/pallas_call | solution.py:355
  4.1 32.2 %all-to-all-start = ((bf16[128,4,128]{2,1,0:T(4,128)(2,1)}), bf16[128,4,128]{2,1,0:T(4,128)(2,1)S(1)}, u32[]{:S(2)}, u32[]{:S(2)}) async-start(bf16[128,4,128]{2,1,0:T(4,128)(2,1)} %bitcast.6), calls=%async_computation | async-start | bytes 262144 | tf_op jit(solution)/shard_map/all_to_all | solution.py:369
  36.3 0.1 collective-permute-start
  36.4 5.0 %collective-permute-start.1 = (bf16[2,72,384]{2,1,0:T(8,128)(2,1)}, bf16[2,72,384]{2,1,0:T(8,128)(2,1)S(1)}, u32[]{:S(2)}, u32[]{:S(2)}) collective-permute-start(bf16[2,72,384]{2,1,0:T(8,128)(2,1)} %get-tuple-element.14), channel_id=1, source_target_pairs={{1,0},{2,1},{3,2},{4,3},{5,4},{6,5},{7,6},{8,7},{9,8},{10,9},{11,1... | collective-permute-start | bytes 331784 | tf_op jit(solution)/shard_map/ppermute | solution.py:368
  41.5 6.1 %combine.1.weight_ref = bf16[2,768,2304]{2,1,0:T(8,128)(2,1)} custom-call(bf16[3,3,3,192,384]{4,3,2,1,0:T(8,128)(2,1)} %bitcast.4), custom_call_target="tpu_custom_call" | custom-call | tf_op jit(solution)/shard_map/combine/pallas_call | solution.py:386
  47.6 0.0 collective-permute-done.before_ref
  47.6 0.0 copy-start.1
  47.6 0.0 collective-permute-done.1.after_ref
  47.6 0.6 copy-done.1
  48.2 0.0 copy-start.2
  48.2 0.7 copy-done.2
  48.9 4.8 %table.1 = (bf16[192,2304]{1,0:T(8,128)(2,1)}, f32[128,128]{1,0:T(8,128)}, bf16[128,128]{1,0:T(8,128)(2,1)}) custom-call(s32[128,768]{1,0:T(8,128)} %layout_ref.3, s32[8]{0:T(128)} %assign_ref.5, bf16[2,4,1024]{2,1,0:T(4,128)(2,1)} %cache_ref.3, bf16[2,72,384]{2,1,0:T(8,128)(2,1)} %copy-done.1, bf16[2,72,384]{2,1,0:T(8,128)(2,1)} %copy-done.2), custom_call_target="tpu_custom_call" | custom-call | tf_op jit(solution)/shard_map/table/pallas_call | solution.py:373
  53.7 0.0 all-to-all-done
  53.8 0.0 copy-start
  53.8 0.6 copy-done
  54.4 13.0 %decode.1 = (bf16[3,8,192,128]{3,2,1,0:T(8,128)(2,1)}, bf16[2,4,1024]{2,1,0:T(4,128)(2,1)}, bf16[2,4,64,384]{3,2,1,0:T(8,128)(2,1)}) custom-call(bf16[512,128]{1,0:T(8,128)(2,1)} %bitcast.5, bf16[192,2304]{1,0:T(8,128)(2,1)} %get-tuple-element.15.hot_ref, f32[128,128]{1,0:T(8,128)} %get-tuple-element.16.code_ref, ...), custom_call_target="tpu_custom_call" | custom-call | tf_op jit(solution)/shard_map/decode/pallas_call | solution.py:395
Async XLA Ops:
  4.1 49.6 %all-to-all-start = ((bf16[128,4,128]{2,1,0:T(4,128)(2,1)}), bf16[128,4,128]{2,1,0:T(4,128)(2,1)S(1)}, u32[]{:S(2)}, u32[]{:S(2)}) async-start(bf16[128,4,128]{2,1,0:T(4,128)(2,1)} %bitcast.6), calls=%async_computation | async-start | bytes 262144 | tf_op jit(solution)/shard_map/all_to_all | solution.py:369
  36.3 11.3 %collective-permute-start = (bf16[2,72,384]{2,1,0:T(8,128)(2,1)}, bf16[2,72,384]{2,1,0:T(8,128)(2,1)S(1)}, u32[]{:S(2)}, u32[]{:S(2)}) collective-permute-start(bf16[2,72,384]{2,1,0:T(8,128)(2,1)} %get-tuple-element.13), channel_id=1, source_target_pairs={{0,1},{1,2},{2,3},{3,4},{4,5},{5,6},{6,7},{7,8},{8,9},{9,10},{10,1... | collective-permute-start | bytes 331784 | tf_op jit(solution)/shard_map/ppermute | solution.py:367
  36.4 11.1 %collective-permute-start.1 = (bf16[2,72,384]{2,1,0:T(8,128)(2,1)}, bf16[2,72,384]{2,1,0:T(8,128)(2,1)S(1)}, u32[]{:S(2)}, u32[]{:S(2)}) collective-permute-start(bf16[2,72,384]{2,1,0:T(8,128)(2,1)} %get-tuple-element.14), channel_id=1, source_target_pairs={{1,0},{2,1},{3,2},{4,3},{5,4},{6,5},{7,6},{8,7},{9,8},{10,9},{11,1... | collective-permute-start | bytes 331784 | tf_op jit(solution)/shard_map/ppermute | solution.py:368
  47.6 0.7 copy-start.1
  48.2 0.7 copy-start.2
  53.8 0.6 copy-start

commit v3 on v2

--- a/solution.py
+++ b/solution.py
@@ -63,7 +63,7 @@
     return (iota((length, length), 0) < iota((length, length), 1)).astype(F32).astype(BF16)
 
 
-def send_kernel(layout_ref, latents_ref, assign_ref, features_ref, cache_ref, out_ref, last_ref, first_ref, rows, wide, sems):
+def send_kernel(layout_ref, latents_hbm, assign_ref, features_ref, cache_hbm, out_ref, last_ref, first_ref, rows, latents_ref, cache_ref, wide, sems):
     devices, slots = layout_ref.shape
     per_peer = slots // devices
     me = lax.axis_index("seq")
@@ -72,9 +72,14 @@
         pltpu.make_async_copy(layout_ref.at[pl.ds(base, 8)], rows, sems.at[0]),
         pltpu.make_async_copy(features_ref.at[:, ROWS_DEV - 1], last_ref.at[:, 0:W], sems.at[1]),
         pltpu.make_async_copy(features_ref.at[:, 0], first_ref.at[:, 0:W], sems.at[2]),
+        pltpu.make_async_copy(latents_hbm, latents_ref, sems.at[3]),
+        pltpu.make_async_copy(cache_hbm, cache_ref, sems.at[4]),
     ]
     for copy in copies:
         copy.start()
+    order = earlier(slots)
+    wide[...] = jnp.zeros(wide.shape, F32)
+    copies[4].wait()
     for ref, top in ((last_ref, ROWS_DEV - HALO), (first_ref, 0)):
         for f in range(2):
             ref[f, W:, :] = jnp.zeros((ref.shape[1] - W, MID_CH), BF16)
@@ -82,13 +87,12 @@
                 for p, (low, high) in enumerate(PIECES):
                     at = W + y * len(PIECES) + p
                     ref[f, at : at + 1, 0 : high - low] = cache_ref[f, top + y : top + y + 1, low:high]
-    order = earlier(slots)
-    wide[...] = jnp.zeros(wide.shape, F32)
     copies[0].wait()
     own = jnp.sum(jnp.where(iota(rows.shape, 0) == me - base, rows[...], 0), axis=0, keepdims=True)
     target = cell_parts(own, assign_ref, devices)[0]
     member = (iota((devices, slots), 0) == target).astype(F32)
     rank = dot(member.astype(BF16), order)
+    copies[3].wait()
     latents = latents_ref[...]
     out = jnp.zeros((devices, LANES), F32)
     for k in range(per_peer):
@@ -110,7 +114,7 @@
     return jnp.concatenate(parts, axis=1)
 
 
-def table_kernel(layout_ref, assign_ref, cache_ref, before_ref, after_ref, hot_ref, code_ref, cached_ref, spread):
+def table_kernel(layout_ref, assign_ref, cache_ref, before_ref, after_ref, across_ref, code_ref, cached_ref, spread):
     devices, slots = layout_ref.shape
     per_group = devices // REQS
     per_peer = slots // devices
@@ -136,10 +140,7 @@
             one = jnp.sum(jnp.where(rank == float(k), code, 0.0), axis=1, keepdims=True)
             codes = jnp.where(lane == j * per_peer + k, one, codes)
     code_ref[...] = codes
-    across = jnp.transpose(codes).astype(I32) & 255
-    for jk in range(TILES * per_peer):
-        hot = (iota((FX, devices), 0) == across[jk : jk + 1, :]).astype(F32)
-        hot_ref[:, jk * devices : (jk + 1) * devices] = hot.astype(BF16)
+    across_ref[...] = jnp.transpose(codes).astype(I32) & 255
     width = W * LAT_CH
     keep = iota((W, width), 1) // LAT_CH == iota((W, width), 0)
     repeat = ((iota((width, LANES), 0) & (LAT_CH - 1)) == (iota((width, LANES), 1) & (LAT_CH - 1))).astype(F32).astype(BF16)
@@ -162,13 +163,26 @@
         cached_ref[f * W : (f + 1) * W, :] = total.astype(BF16)
 
 
-def weight_kernel(weight_ref, out_ref):
-    taps = [[weight_ref[0, b, e].astype(F32) for e in range(3)] for b in range(3)]
-    for a, i, rows in ((0, 0, (0,)), (0, 1, (1, 2)), (1, 0, (0, 1)), (1, 1, (2,))):
-        line = [sum(taps[b][e] for b in rows[1:]) + taps[rows[0]][e] if len(rows) > 1 else taps[rows[0]][e] for e in range(3)]
-        parts = (line[1] + line[2], line[0] + line[1], line[0], line[2])
-        for g, part in enumerate(parts):
-            out_ref[a, g * OUT_CH : (g + 1) * OUT_CH, i * MID_CH : (i + 1) * MID_CH] = part.astype(BF16)
+def weight_kernel(weight_ref, out_ref, raw, sums, sems, out_sems):
+    copies = [pltpu.make_async_copy(weight_ref.at[tau], raw.at[tau], sems.at[tau]) for tau in range(3)]
+    for copy in copies:
+        copy.start()
+    sends = []
+    for tau in range(3):
+        copies[tau].wait()
+        lanes = pl.ds(tau * 2 * MID_CH, 2 * MID_CH)
+        for a in range(2):
+            for i, rows in enumerate((((0,), (1, 2)), ((0, 1), (2,)))[a]):
+                line = [sum((raw[tau, b, e].astype(F32) for b in rows[1:]), raw[tau, rows[0], e].astype(F32)) for e in range(3)]
+                parts = (line[1] + line[2], line[0] + line[1], line[0], line[2])
+                at = (tau * 2 + i) * MID_CH
+                for g, part in enumerate(parts):
+                    sums[a, g * OUT_CH : (g + 1) * OUT_CH, at : at + MID_CH] = part.astype(BF16)
+            send = pltpu.make_async_copy(sums.at[a, :, lanes], out_ref.at[a, :, lanes], out_sems.at[tau * 2 + a])
+            send.start()
+            sends.append(send)
+    for send in sends:
+        send.wait()
 
 
 def shifted(values, step, columns):
@@ -183,12 +197,12 @@
 
 def decode_kernel(
     incoming_ref,
-    hot_ref,
+    across_ref,
     code_ref,
     cached_ref,
     assign_ref,
     counts_ref,
-    first_weight_ref,
+    first_hbm,
     first_bias_ref,
     gain_ref,
     second_bias_ref,
@@ -199,6 +213,8 @@
     out_ref,
     latent_ref,
     next_ref,
+    first_weight_ref,
+    weave_ref,
     weight,
     second,
     padded,
@@ -218,23 +234,24 @@
     live = counts_ref[assign_ref[place // per_group]]
     copies = [
         pltpu.make_async_copy(features_ref, second.at[0:2, 1 : 1 + ROWS_DEV], sems.at[0]),
-        pltpu.make_async_copy(before_ref.at[:, 0:W], second.at[0:2, 0], sems.at[1]),
-        pltpu.make_async_copy(after_ref.at[:, 0:W], second.at[0:2, MID_ROWS - 1], sems.at[2]),
-        pltpu.make_async_copy(weight_ref, weight, sems.at[3]),
+        pltpu.make_async_copy(first_hbm, first_weight_ref, sems.at[1]),
+        pltpu.make_async_copy(weight_ref.at[0], weight.at[0], sems.at[2]),
+        pltpu.make_async_copy(weight_ref.at[1], weight.at[1], sems.at[3]),
     ]
     for copy in copies:
         copy.start()
 
-    margin = (WIN_ROWS - 3) * LAT_CH
-    for a in range(3):
-        for e in range(3):
-            padded[a * 3 + e, 0:margin, :] = jnp.zeros((margin, MID_CH), BF16)
-            padded[a * 3 + e, margin + 3 * LAT_CH :, :] = jnp.zeros((margin, MID_CH), BF16)
-            for b in range(3):
-                padded[a * 3 + e, margin + b * LAT_CH : margin + (b + 1) * LAT_CH, :] = first_weight_ref[a, b, e]
-
-    pairs = hot_ref.shape[1] // devices
-    per_peer = pairs // TILES
+    half = 2 * W
+    at = iota((2 * half, 2 * half), 0)
+    source_row = (at & (half - 1)) // W
+    target = (at & (W - 1)) * 2 + at // half + source_row * half
+    weave_ref[...] = (target == iota((2 * half, 2 * half), 1)).astype(F32).astype(BF16)
+
+    per_peer = FX * ROWS_DEV // devices
+    pairs = TILES * per_peer
+    hot = jnp.concatenate(
+        [(iota((FX, devices), 0) == across_ref[jk : jk + 1, :]).astype(F32).astype(BF16) for jk in range(pairs)], axis=1
+    )
     wide = per_peer * LANES
     source = iota((LANES, wide), 1)
     expand = (iota((LANES, wide), 0) == source // LANES * LAT_CH + (source & (LAT_CH - 1))).astype(F32).astype(BF16)
@@ -247,10 +264,19 @@
             jk = j * per_peer + k
             part = jnp.where(lane == codes[:, jk : jk + 1], spread[:, k * LANES : (k + 1) * LANES], 0.0)
             cells[jk * devices : (jk + 1) * devices, :] = part.astype(BF16)
-    arranged = dot(hot_ref[...], cells[...])
+    arranged = dot(hot, cells[...])
     frames = jnp.concatenate([cached_ref[...].astype(F32), arranged], axis=0)
     for e in range(3):
         window[e] = shifted(frames, e, W).astype(BF16)
+
+    copies[1].wait()
+    margin = (WIN_ROWS - 3) * LAT_CH
+    for a in range(3):
+        for e in range(3):
+            padded[a * 3 + e, 0:margin, :] = jnp.zeros((margin, MID_CH), BF16)
+            padded[a * 3 + e, margin + 3 * LAT_CH :, :] = jnp.zeros((margin, MID_CH), BF16)
+            for b in range(3):
+                padded[a * 3 + e, margin + b * LAT_CH : margin + (b + 1) * LAT_CH, :] = first_weight_ref[a, b, e]
 
     taps = jnp.concatenate([window[e, a * W : a * W + FX, :] for a in range(3) for e in range(3)], axis=1)
     for r in range(MID_ROWS):
@@ -266,17 +292,12 @@
             active = jnp.where(position == per_group - 1, 0.0, active)
         for t in range(FMAX):
             second[2 + t, r] = active[t * W : (t + 1) * W, :].astype(BF16)
-    for copy in copies:
-        copy.wait()
-
-    @pl.when(position == 0)
-    def _():
-        second[0:2, 0] = jnp.zeros((2, W, MID_CH), BF16)
-
-    @pl.when(position == per_group - 1)
-    def _():
-        second[0:2, MID_ROWS - 1] = jnp.zeros((2, W, MID_CH), BF16)
-
+    for f in range(2):
+        edge = before_ref[f, 0:W, :]
+        second[f, 0] = jnp.where(position == 0, jnp.zeros_like(edge), edge)
+        edge = after_ref[f, 0:W, :]
+        second[f, MID_ROWS - 1] = jnp.where(position == per_group - 1, jnp.zeros_like(edge), edge)
+    copies[0].wait()
     ahead = pltpu.make_async_copy(second.at[pl.ds(live, 2), 1 : 1 + ROWS_DEV], next_ref, sems.at[0])
     ahead.start()
 
@@ -289,13 +310,22 @@
         for f in range(2):
             latent_ref[f, y : y + 1, :] = jnp.sum(flat[f * W : (f + 1) * W], axis=0, keepdims=True).astype(BF16)
 
-    half = 2 * W
     pixels = ROWS_DEV * W
     diagonal = iota((OUT_CH, OUT_CH), 0) == iota((OUT_CH, OUT_CH), 1)
     bias = jnp.sum(jnp.where(diagonal, second_bias_ref[...][None, :], 0.0), axis=1, keepdims=True)
     column = iota((OUT_CH, pixels), 1) & (W - 1)
-    for t in range(FMAX):
-        for a in range(2):
+    def interleave(a):
+        woven = dot(halves[a], weave_ref[...]).astype(BF16)
+        for t in range(FMAX):
+            for pair in range(ROWS_DEV // 2):
+                start = (t * (ROWS_DEV // 2) + pair) * OUT_CH
+                for y in range(2):
+                    decoded[a, t, 2 * pair + y] = woven[start : start + OUT_CH, y * half : (y + 1) * half]
+        pltpu.make_async_copy(decoded.at[a], out_ref.at[:, :, a], out_sems.at[a]).start()
+
+    for a in range(2):
+        copies[2 + a].wait()
+        for t in range(FMAX):
             block = jnp.concatenate(
                 [second[t + tau, a + i : a + i + ROWS_DEV].reshape(pixels, MID_CH) for tau in range(3) for i in range(2)],
                 axis=1,
@@ -309,26 +339,17 @@
             odd = jnp.where(t < live, odd, 0.0).astype(BF16)
             for pair in range(ROWS_DEV // 2):
                 lanes = slice(pair * half, (pair + 1) * half)
-                at = (pair * 2 + a) * OUT_CH
-                halves[t, at : at + OUT_CH, 0:half] = even[:, lanes]
-                halves[t, at : at + OUT_CH, half : 2 * half] = odd[:, lanes]
-
-    @pl.loop(0, FMAX)
-    def _(t):
-        at = iota((2 * half, 2 * half), 0)
-        to = iota((2 * half, 2 * half), 1)
-        source_row = (at & (half - 1)) // W
-        weave = ((at & (W - 1)) * 2 + at // half + source_row * half == to).astype(F32).astype(BF16)
-        woven = dot(halves[t], weave).astype(BF16)
-        for pair in range(ROWS_DEV // 2):
-            for a in range(2):
-                start = (pair * 2 + a) * OUT_CH
-                for y in range(2):
-                    decoded[t, 2 * (2 * pair + y) + a] = woven[start : start + OUT_CH, y * half : (y + 1) * half]
-        pltpu.make_async_copy(decoded.at[t], out_ref.at[t], out_sems.at[0]).start()
-
-    pltpu.make_async_copy(decoded, out_ref, out_sems.at[0]).wait()
+                start = (t * (ROWS_DEV // 2) + pair) * OUT_CH
+                halves[a, start : start + OUT_CH, 0:half] = even[:, lanes]
+                halves[a, start : start + OUT_CH, half : 2 * half] = odd[:, lanes]
+        pl.when(live >= 0)(lambda a=a: interleave(a))
+    for a in range(2):
+        pltpu.make_async_copy(decoded.at[a], out_ref.at[:, :, a], out_sems.at[a]).wait()
     ahead.wait()
+
+
+def in_vmem(array):
+    return pltpu.with_memory_space_constraint(array, pltpu.VMEM)
 
 
 def body(
@@ -355,27 +376,29 @@
     outgoing, last, first = pl.pallas_call(
         send_kernel,
         out_shape=(jax.ShapeDtypeStruct((devices * SLOTS, LANES), BF16), edge, edge),
-        in_specs=[ANY, VMEM, SMEM, ANY, VMEM],
+        in_specs=[ANY, ANY, SMEM, ANY, ANY],
         out_specs=(VMEM, VMEM, VMEM),
         scratch_shapes=[
             pltpu.VMEM((8, slots), I32),
+            pltpu.VMEM(latents.shape, BF16),
+            pltpu.VMEM(latent_cache.shape, BF16),
             pltpu.VMEM((devices * SLOTS, LANES), F32),
-            pltpu.SemaphoreType.DMA((3,)),
+            pltpu.SemaphoreType.DMA((5,)),
         ],
         name="send",
     )(layout, latents, assign, feature_cache, latent_cache)
-    before = lax.ppermute(last, "seq", up)
-    after = lax.ppermute(first, "seq", down)
+    before = in_vmem(lax.ppermute(last, "seq", up))
+    after = in_vmem(lax.ppermute(first, "seq", down))
     incoming = lax.all_to_all(
         outgoing.reshape(devices, SLOTS, LANES), "seq", split_axis=0, concat_axis=0, tiled=True
     ).reshape(devices * SLOTS, LANES)
 
-    hot, codes, cached = pl.pallas_call(
+    across, codes, cached = pl.pallas_call(
         table_kernel,
         out_shape=(
-            jax.ShapeDtypeStruct((FX, pairs * devices), BF16),
-            jax.ShapeDtypeStruct((devices, LANES), F32),
-            jax.ShapeDtypeStruct((2 * W, LANES), BF16),
+            pltpu.VMEM((LANES, devices), I32),
+            pltpu.VMEM((devices, LANES), F32),
+            pltpu.VMEM((2 * W, LANES), BF16),
         ),
         in_specs=[VMEM, SMEM, VMEM, VMEM, VMEM],
         out_specs=(VMEM, VMEM, VMEM),
@@ -385,40 +408,47 @@
 
     combined = pl.pallas_call(
         weight_kernel,
-        grid=(3,),
         out_shape=jax.ShapeDtypeStruct((2, 4 * OUT_CH, 6 * MID_CH), BF16),
-        in_specs=[pl.BlockSpec((1, 3, 3, OUT_CH, MID_CH), lambda t: (t, 0, 0, 0, 0))],
-        out_specs=pl.BlockSpec((2, 4 * OUT_CH, 2 * MID_CH), lambda t: (0, 0, t)),
+        in_specs=[ANY],
+        out_specs=ANY,
+        scratch_shapes=[
+            pltpu.VMEM((3, 3, 3, OUT_CH, MID_CH), BF16),
+            pltpu.VMEM((2, 4 * OUT_CH, 6 * MID_CH), BF16),
+            pltpu.SemaphoreType.DMA((3,)),
+            pltpu.SemaphoreType.DMA((6,)),
+        ],
         name="combine",
     )(jnp.swapaxes(second_weight, 3, 4))
 
     decoded, latent_next, feature_next = pl.pallas_call(
         decode_kernel,
         out_shape=(
-            jax.ShapeDtypeStruct((FMAX, 2 * ROWS_DEV, OUT_CH, 2 * W), BF16),
+            jax.ShapeDtypeStruct((FMAX, ROWS_DEV, 2, OUT_CH, 2 * W), BF16),
             jax.ShapeDtypeStruct((2, ROWS_DEV, W * LAT_CH), BF16),
             jax.ShapeDtypeStruct((2, ROWS_DEV, W, MID_CH), BF16),
         ),
-        in_specs=[VMEM] * 4 + [SMEM] * 2 + [VMEM] * 4 + [ANY] * 4,
+        in_specs=[VMEM] * 4 + [SMEM] * 2 + [ANY] + [VMEM] * 3 + [ANY] + [VMEM] * 2 + [ANY],
         out_specs=(ANY, VMEM, ANY),
         scratch_shapes=[
+            pltpu.VMEM(first_weight.shape, BF16),
+            pltpu.VMEM((4 * W, 4 * W), BF16),
             pltpu.VMEM((2, 4 * OUT_CH, 6 * MID_CH), BF16),
             pltpu.VMEM((5, MID_ROWS, W, MID_CH), BF16),
             pltpu.VMEM((9, (2 * WIN_ROWS - 3) * LAT_CH, MID_CH), BF16),
             pltpu.VMEM((pairs * devices, LANES), BF16),
             pltpu.VMEM((3, 5 * W, LANES), BF16),
             pltpu.VMEM((devices * SLOTS, LANES), F32),
-            pltpu.VMEM((FMAX, ROWS_DEV * OUT_CH, 4 * W), BF16),
-            pltpu.VMEM((FMAX, 2 * ROWS_DEV, OUT_CH, 2 * W), BF16),
+            pltpu.VMEM((2, FMAX * (ROWS_DEV // 2) * OUT_CH, 4 * W), BF16),
+            pltpu.VMEM((2, FMAX, ROWS_DEV, OUT_CH, 2 * W), BF16),
             pltpu.SemaphoreType.DMA((4,)),
-            pltpu.SemaphoreType.DMA((1,)),
+            pltpu.SemaphoreType.DMA((2,)),
         ],
         name="decode",
     )(
-        incoming,
-        hot,
-        codes,
-        cached,
+        in_vmem(incoming),
+        in_vmem(across),
+        in_vmem(codes),
+        in_vmem(cached),
         assign,
         counts,
         first_weight,
@@ -430,6 +460,7 @@
         after,
         combined,
     )
+    decoded = decoded.reshape(FMAX, 2 * ROWS_DEV, OUT_CH, 2 * W)
     return (jnp.swapaxes(decoded, 2, 3), latent_next, feature_next)
 
 

time: 67.9 us -> 64.3 us (0.947); the launches traced: 67.6 us -> 63.1 us
  Pallas kernels: 27.4 us -> 24.6 us
  local copies, waits for them, and re-layouts: 1.96 us -> 0 us
    pallas_call x3, Pallas kernels: 23.9 us -> 20.9 us  [the longest x1 12.7 us: body(): pl.pallas_call(decode_kernel, out_shape=(jax.ShapeDtypeStruct((FMAX, ROWS...]
    unnamed x6 -> x0, local copies, waits for them, and re-layouts: 1.96 us -> none
  transfers between devices with their start and end apart: 3 -> 3, of which waited for: 0 -> 1; matrix products, arithmetic and copies ran while one was open for 0% -> 0% of each run, Pallas kernels for 16% -> 13%
where the time goes in v3:
time: 64.3 us; the launch traced here: 63.1 us
  starting transfers between devices  37.3 us (58%)
  Pallas kernels  24.6 us (38%)
  between operations  0.84 us (1%)
    all_to_all x1, starting transfers between devices, body(): lax.all_to_all(outgoing.reshape(devices, SLOTS, LANES), 'seq', split_axis...  32.2 us
    pallas_call x1, Pallas kernels, body(): pl.pallas_call(decode_kernel, out_shape=(jax.ShapeDtypeStruct((FMAX, ROWS...  12.7 us
    ppermute x1, starting transfers between devices, body(): after = in_vmem(lax.ppermute(first, 'seq', down))  5.04 us
    pallas_call x1, Pallas kernels, body(): pl.pallas_call(weight_kernel, out_shape=jax.ShapeDtypeStruct((2, 4 * OUT_...  4.6 us
    pallas_call x1, Pallas kernels, body(): pl.pallas_call(send_kernel, out_shape=(jax.ShapeDtypeStruct((devices * SL...  3.7 us
    pallas_call x1, Pallas kernels, body(): pl.pallas_call(table_kernel, out_shape=(pltpu.VMEM((LANES, devices), I32)...  3.65 us
  transfers between devices with their start and end apart: 3, of which 1 were waited for; matrix products, arithmetic and copies ran while one was open for 0% of the time, Pallas kernels for 13%

profile of v3, /device:TPU:40, one launch (start us, length us, event | category | flops | bytes accessed | tf_op | source)
XLA Modules:
  0.0 63.1 jit_solution(14270131008762083163)
XLA Ops:
  0.6 3.7 %send.1 = (bf16[512,128]{1,0:T(8,128)(2,1)}, bf16[2,72,384]{2,1,0:T(8,128)(2,1)}, bf16[2,72,384]{2,1,0:T(8,128)(2,1)}) custom-call(s32[128,768]{1,0:T(8,128)} %layout_ref.3, bf16[16,768]{1,0:T(8,128)(2,1)} %latents_hbm.1, s32[8]{0:T(128)} %assign_ref.5, bf16[2,4,64,384]{3,2,1,0:T(8,128)(2,1)} %features_ref.3, bf16[2,4,1024]{2,1,0:T(4,128)(2,1)} %cache_ref.1), custom_call_target="tpu_custom_call" | custom-call | tf_op jit(solution)/shard_map/send/pallas_call | solution.py:376
  4.3 32.2 %all-to-all-start = ((bf16[128,4,128]{2,1,0:T(4,128)(2,1)}), bf16[128,4,128]{2,1,0:T(4,128)(2,1)S(1)}, u32[]{:S(2)}, u32[]{:S(2)}) async-start(bf16[128,4,128]{2,1,0:T(4,128)(2,1)} %bitcast.8), calls=%async_computation | async-start | bytes 262144 | tf_op jit(solution)/shard_map/all_to_all | solution.py:392
  36.5 0.1 collective-permute-start
  36.6 5.0 %collective-permute-start.1 = (bf16[2,72,384]{2,1,0:T(8,128)(2,1)}, bf16[2,72,384]{2,1,0:T(8,128)(2,1)S(1)}, u32[]{:S(2)}, u32[]{:S(2)}) collective-permute-start(bf16[2,72,384]{2,1,0:T(8,128)(2,1)} %get-tuple-element.14), channel_id=1, source_target_pairs={{1,0},{2,1},{3,2},{4,3},{5,4},{6,5},{7,6},{8,7},{9,8},{10,9},{11,1... | collective-permute-start | bytes 331784 | tf_op jit(solution)/shard_map/ppermute | solution.py:391
  41.7 4.6 %combine.1.weight_ref = bf16[2,768,2304]{2,1,0:T(8,128)(2,1)} custom-call(bf16[3,3,3,192,384]{4,3,2,1,0:T(8,128)(2,1)} %bitcast.7), custom_call_target="tpu_custom_call" | custom-call | tf_op jit(solution)/shard_map/combine/pallas_call | solution.py:409
  46.3 0.3 collective-permute-done.before_ref
  46.6 0.0 collective-permute-done.1.after_ref
  46.6 3.6 %table.1 = (s32[128,128]{1,0:T(8,128)S(1)}, f32[128,128]{1,0:T(8,128)S(1)}, bf16[128,128]{1,0:T(8,128)(2,1)S(1)}) custom-call(s32[128,768]{1,0:T(8,128)} %layout_ref.3, s32[8]{0:T(128)} %assign_ref.5, bf16[2,4,1024]{2,1,0:T(4,128)(2,1)} %cache_ref.1, bf16[2,72,384]{2,1,0:T(8,128)(2,1)S(1)} %collective-permute-done.before_ref, ...), custom_call_target="tpu_custom_call" | custom-call | tf_op jit(solution)/shard_map/table/pallas_call | solution.py:396
  50.2 0.0 all-to-all-done
  50.2 12.7 %decode.1 = (bf16[3,4,2,192,128]{4,3,2,1,0:T(8,128)(2,1)}, bf16[2,4,1024]{2,1,0:T(4,128)(2,1)}, bf16[2,4,64,384]{3,2,1,0:T(8,128)(2,1)}) custom-call(bf16[512,128]{1,0:T(8,128)(2,1)S(1)} %bitcast.6, s32[128,128]{1,0:T(8,128)S(1)} %get-tuple-element.15.across_ref, f32[128,128]{1,0:T(8,128)S(1)} %get-tuple-element.16.code_ref, ...), custom_call_target="tpu_custom_call" | custom-call | tf_op jit(solution)/shard_map/decode/pallas_call | solution.py:423
Async XLA Ops:
  4.3 45.9 %all-to-all-start = ((bf16[128,4,128]{2,1,0:T(4,128)(2,1)}), bf16[128,4,128]{2,1,0:T(4,128)(2,1)S(1)}, u32[]{:S(2)}, u32[]{:S(2)}) async-start(bf16[128,4,128]{2,1,0:T(4,128)(2,1)} %bitcast.8), calls=%async_computation | async-start | bytes 262144 | tf_op jit(solution)/shard_map/all_to_all | solution.py:392
  36.5 10.1 %collective-permute-start = (bf16[2,72,384]{2,1,0:T(8,128)(2,1)}, bf16[2,72,384]{2,1,0:T(8,128)(2,1)S(1)}, u32[]{:S(2)}, u32[]{:S(2)}) collective-permute-start(bf16[2,72,384]{2,1,0:T(8,128)(2,1)} %get-tuple-element.13), channel_id=1, source_target_pairs={{0,1},{1,2},{2,3},{3,4},{4,5},{5,6},{6,7},{7,8},{8,9},{9,10},{10,1... | collective-permute-start | bytes 331784 | tf_op jit(solution)/shard_map/ppermute | solution.py:390
  36.6 9.9 %collective-permute-start.1 = (bf16[2,72,384]{2,1,0:T(8,128)(2,1)}, bf16[2,72,384]{2,1,0:T(8,128)(2,1)S(1)}, u32[]{:S(2)}, u32[]{:S(2)}) collective-permute-start(bf16[2,72,384]{2,1,0:T(8,128)(2,1)} %get-tuple-element.14), channel_id=1, source_target_pairs={{1,0},{2,1},{3,2},{4,3},{5,4},{6,5},{7,6},{8,7},{9,8},{10,9},{11,1... | collective-permute-start | bytes 331784 | tf_op jit(solution)/shard_map/ppermute | solution.py:391

commit v4 on v3

--- a/solution.py
+++ b/solution.py
@@ -47,13 +47,12 @@
     column = numbers & (W - 1)
     image_row = (numbers >> w_bits) & (height - 1)
     frames = numbers >> (w_bits + h_bits)
-    request = jnp.zeros_like(frames)
-    for r in range(1, REQS):
-        request = request + (frames >= r * FMAX).astype(I32)
+    request = (frames * 11) >> 5
     frame = frames - request * FMAX
-    group = jnp.zeros_like(frames)
+    group_of = jnp.int32(0)
     for g in range(1, REQS):
-        group = jnp.where(request == assign_ref[g], g, group)
+        group_of = group_of + (jnp.int32(g) << (assign_ref[g] * 4))
+    group = (group_of >> (request * 4)) & (REQS - 1)
     place = group * per_group + image_row // ROWS_DEV
     target = (place - per_group // 2 + devices) & (devices - 1)
     return target, frame, image_row & (ROWS_DEV - 1), column
@@ -63,7 +62,9 @@
     return (iota((length, length), 0) < iota((length, length), 1)).astype(F32).astype(BF16)
 
 
-def send_kernel(layout_ref, latents_hbm, assign_ref, features_ref, cache_hbm, out_ref, last_ref, first_ref, rows, latents_ref, cache_ref, wide, sems):
+def send_kernel(
+    layout_ref, latents_hbm, assign_hbm, features_ref, cache_hbm, out_ref, last_ref, first_ref, rows, latents_ref, cache_ref, assign_ref, wide, sems
+):
     devices, slots = layout_ref.shape
     per_peer = slots // devices
     me = lax.axis_index("seq")
@@ -74,6 +75,7 @@
         pltpu.make_async_copy(features_ref.at[:, 0], first_ref.at[:, 0:W], sems.at[2]),
         pltpu.make_async_copy(latents_hbm, latents_ref, sems.at[3]),
         pltpu.make_async_copy(cache_hbm, cache_ref, sems.at[4]),
+        pltpu.make_async_copy(assign_hbm, assign_ref, sems.at[5]),
     ]
     for copy in copies:
         copy.start()
@@ -88,6 +90,7 @@
                     at = W + y * len(PIECES) + p
                     ref[f, at : at + 1, 0 : high - low] = cache_ref[f, top + y : top + y + 1, low:high]
     copies[0].wait()
+    copies[5].wait()
     own = jnp.sum(jnp.where(iota(rows.shape, 0) == me - base, rows[...], 0), axis=0, keepdims=True)
     target = cell_parts(own, assign_ref, devices)[0]
     member = (iota((devices, slots), 0) == target).astype(F32)
@@ -200,12 +203,12 @@
     across_ref,
     code_ref,
     cached_ref,
-    assign_ref,
-    counts_ref,
+    assign_hbm,
+    counts_hbm,
     first_hbm,
-    first_bias_ref,
-    gain_ref,
-    second_bias_ref,
+    first_bias_hbm,
+    gain_hbm,
+    second_bias_hbm,
     features_ref,
     before_ref,
     after_ref,
@@ -213,6 +216,11 @@
     out_ref,
     latent_ref,
     next_ref,
+    assign_ref,
+    counts_ref,
+    first_bias_ref,
+    gain_ref,
+    second_bias_ref,
     first_weight_ref,
     weave_ref,
     weight,
@@ -231,14 +239,18 @@
     me = lax.axis_index("seq")
     place = (me + per_group // 2) & (devices - 1)
     position = place & (per_group - 1)
-    live = counts_ref[assign_ref[place // per_group]]
     copies = [
         pltpu.make_async_copy(features_ref, second.at[0:2, 1 : 1 + ROWS_DEV], sems.at[0]),
         pltpu.make_async_copy(first_hbm, first_weight_ref, sems.at[1]),
         pltpu.make_async_copy(weight_ref.at[0], weight.at[0], sems.at[2]),
         pltpu.make_async_copy(weight_ref.at[1], weight.at[1], sems.at[3]),
+        pltpu.make_async_copy(assign_hbm, assign_ref, sems.at[4]),
+        pltpu.make_async_copy(counts_hbm, counts_ref, sems.at[5]),
+        pltpu.make_async_copy(first_bias_hbm, first_bias_ref, sems.at[6]),
+        pltpu.make_async_copy(gain_hbm, gain_ref, sems.at[7]),
+        pltpu.make_async_copy(second_bias_hbm, second_bias_ref, sems.at[8]),
     ]
-    for copy in copies:
+    for copy in copies[4:] + copies[1:2] + copies[0:1] + copies[2:4]:
         copy.start()
 
     half = 2 * W
@@ -269,7 +281,9 @@
     for e in range(3):
         window[e] = shifted(frames, e, W).astype(BF16)
 
-    copies[1].wait()
+    for copy in copies[4:] + copies[1:2]:
+        copy.wait()
+    live = counts_ref[assign_ref[place // per_group]]
     margin = (WIN_ROWS - 3) * LAT_CH
     for a in range(3):
         for e in range(3):
@@ -376,14 +390,15 @@
     outgoing, last, first = pl.pallas_call(
         send_kernel,
         out_shape=(jax.ShapeDtypeStruct((devices * SLOTS, LANES), BF16), edge, edge),
-        in_specs=[ANY, ANY, SMEM, ANY, ANY],
+        in_specs=[ANY] * 5,
         out_specs=(VMEM, VMEM, VMEM),
         scratch_shapes=[
             pltpu.VMEM((8, slots), I32),
             pltpu.VMEM(latents.shape, BF16),
             pltpu.VMEM(latent_cache.shape, BF16),
+            pltpu.SMEM(assign.shape, I32),
             pltpu.VMEM((devices * SLOTS, LANES), F32),
-            pltpu.SemaphoreType.DMA((5,)),
+            pltpu.SemaphoreType.DMA((6,)),
         ],
         name="send",
     )(layout, latents, assign, feature_cache, latent_cache)
@@ -427,9 +442,14 @@
             jax.ShapeDtypeStruct((2, ROWS_DEV, W * LAT_CH), BF16),
             jax.ShapeDtypeStruct((2, ROWS_DEV, W, MID_CH), BF16),
         ),
-        in_specs=[VMEM] * 4 + [SMEM] * 2 + [ANY] + [VMEM] * 3 + [ANY] + [VMEM] * 2 + [ANY],
+        in_specs=[VMEM] * 4 + [ANY] * 7 + [VMEM] * 2 + [ANY],
         out_specs=(ANY, VMEM, ANY),
         scratch_shapes=[
+            pltpu.SMEM(assign.shape, I32),
+            pltpu.SMEM(counts.shape, I32),
+            pltpu.VMEM(first_bias.shape, F32),
+            pltpu.VMEM(norm_gain.shape, F32),
+            pltpu.VMEM(second_bias.shape, F32),
             pltpu.VMEM(first_weight.shape, BF16),
             pltpu.VMEM((4 * W, 4 * W), BF16),
             pltpu.VMEM((2, 4 * OUT_CH, 6 * MID_CH), BF16),
@@ -440,7 +460,7 @@
             pltpu.VMEM((devices * SLOTS, LANES), F32),
             pltpu.VMEM((2, FMAX * (ROWS_DEV // 2) * OUT_CH, 4 * W), BF16),
             pltpu.VMEM((2, FMAX, ROWS_DEV, OUT_CH, 2 * W), BF16),
-            pltpu.SemaphoreType.DMA((4,)),
+            pltpu.SemaphoreType.DMA((9,)),
             pltpu.SemaphoreType.DMA((2,)),
         ],
         name="decode",

time: 64.3 us -> 62.8 us (0.977)
  Pallas kernels: 24.6 us -> 22.7 us
    pallas_call x1, Pallas kernels: 12.7 us -> 11.9 us  [body(): pl.pallas_call(decode_kernel, out_shape=(jax.ShapeDtypeStruct((FMAX, ROWS...]
    pallas_call x1, Pallas kernels: 3.7 us -> 3.04 us  [body(): pl.pallas_call(send_kernel, out_shape=(jax.ShapeDtypeStruct((devices * SL...]
  transfers between devices with their start and end apart: 3 -> 3, of which waited for: 1 -> 2; matrix products, arithmetic and copies ran while one was open for 0% -> 0% of each run, Pallas kernels for 13% -> 13%
where the time goes in v4:
time: 62.8 us; the launch traced here: 61.6 us
  starting transfers between devices  37.3 us (59%)
  Pallas kernels  22.7 us (36%)
  between operations  0.83 us (1%)
  waiting for transfers between devices  0.66 us (1%)
    all_to_all x1, starting transfers between devices, body(): lax.all_to_all(outgoing.reshape(devices, SLOTS, LANES), 'seq', split_axis...  32.2 us
    pallas_call x1, Pallas kernels, body(): pl.pallas_call(decode_kernel, out_shape=(jax.ShapeDtypeStruct((FMAX, ROWS...  11.9 us
    ppermute x1, starting transfers between devices, body(): after = in_vmem(lax.ppermute(first, 'seq', down))  5.04 us
    pallas_call x1, Pallas kernels, body(): pl.pallas_call(weight_kernel, out_shape=jax.ShapeDtypeStruct((2, 4 * OUT_...  4.6 us
    pallas_call x1, Pallas kernels, body(): pl.pallas_call(table_kernel, out_shape=(pltpu.VMEM((LANES, devices), I32)...  3.2 us
    pallas_call x1, Pallas kernels, body(): pl.pallas_call(send_kernel, out_shape=(jax.ShapeDtypeStruct((devices * SL...  3.04 us
  transfers between devices with their start and end apart: 3, of which 2 were waited for; matrix products, arithmetic and copies ran while one was open for 0% of the time, Pallas kernels for 13%

profile of v4, /device:TPU:40, one launch (start us, length us, event | category | flops | bytes accessed | tf_op | source)
XLA Modules:
  0.0 61.6 jit_solution(6928732350122719503)
XLA Ops:
  0.6 3.0 %send.1 = (bf16[512,128]{1,0:T(8,128)(2,1)}, bf16[2,72,384]{2,1,0:T(8,128)(2,1)}, bf16[2,72,384]{2,1,0:T(8,128)(2,1)}) custom-call(s32[128,768]{1,0:T(8,128)} %layout_ref.3, bf16[16,768]{1,0:T(8,128)(2,1)} %latents_hbm.1, s32[8]{0:T(128)} %assign_hbm.3, bf16[2,4,64,384]{3,2,1,0:T(8,128)(2,1)} %features_ref.3, bf16[2,4,1024]{2,1,0:T(4,128)(2,1)} %cache_ref.1), custom_call_target="tpu_custom_call" | custom-call | tf_op jit(solution)/shard_map/send/pallas_call | solution.py:390
  3.7 32.2 %all-to-all-start = ((bf16[128,4,128]{2,1,0:T(4,128)(2,1)}), bf16[128,4,128]{2,1,0:T(4,128)(2,1)S(1)}, u32[]{:S(2)}, u32[]{:S(2)}) async-start(bf16[128,4,128]{2,1,0:T(4,128)(2,1)} %bitcast.8), calls=%async_computation | async-start | bytes 262144 | tf_op jit(solution)/shard_map/all_to_all | solution.py:407
  35.9 0.1 collective-permute-start
  36.0 5.0 %collective-permute-start.1 = (bf16[2,72,384]{2,1,0:T(8,128)(2,1)}, bf16[2,72,384]{2,1,0:T(8,128)(2,1)S(1)}, u32[]{:S(2)}, u32[]{:S(2)}) collective-permute-start(bf16[2,72,384]{2,1,0:T(8,128)(2,1)} %get-tuple-element.14), channel_id=1, source_target_pairs={{1,0},{2,1},{3,2},{4,3},{5,4},{6,5},{7,6},{8,7},{9,8},{10,9},{11,1... | collective-permute-start | bytes 331784 | tf_op jit(solution)/shard_map/ppermute | solution.py:406
  41.0 4.6 %combine.1.weight_ref = bf16[2,768,2304]{2,1,0:T(8,128)(2,1)} custom-call(bf16[3,3,3,192,384]{4,3,2,1,0:T(8,128)(2,1)} %bitcast.7), custom_call_target="tpu_custom_call" | custom-call | tf_op jit(solution)/shard_map/combine/pallas_call | solution.py:424
  45.6 0.3 collective-permute-done.before_ref
  45.9 0.0 collective-permute-done.1.after_ref
  45.9 3.2 %table.1 = (s32[128,128]{1,0:T(8,128)S(1)}, f32[128,128]{1,0:T(8,128)S(1)}, bf16[128,128]{1,0:T(8,128)(2,1)S(1)}) custom-call(s32[128,768]{1,0:T(8,128)} %layout_ref.3, s32[8]{0:T(128)} %assign_hbm.3, bf16[2,4,1024]{2,1,0:T(4,128)(2,1)} %cache_ref.1, bf16[2,72,384]{2,1,0:T(8,128)(2,1)S(1)} %collective-permute-done.before_ref, ...), custom_call_target="tpu_custom_call" | custom-call | tf_op jit(solution)/shard_map/table/pallas_call | solution.py:411
  49.1 0.4 all-to-all-done
  49.5 11.9 %decode.1 = (bf16[3,4,2,192,128]{4,3,2,1,0:T(8,128)(2,1)}, bf16[2,4,1024]{2,1,0:T(4,128)(2,1)}, bf16[2,4,64,384]{3,2,1,0:T(8,128)(2,1)}) custom-call(bf16[512,128]{1,0:T(8,128)(2,1)S(1)} %bitcast.6, s32[128,128]{1,0:T(8,128)S(1)} %get-tuple-element.15.across_ref, f32[128,128]{1,0:T(8,128)S(1)} %get-tuple-element.16.code_ref, ...), custom_call_target="tpu_custom_call" | custom-call | tf_op jit(solution)/shard_map/decode/pallas_call | solution.py:438
Async XLA Ops:
  3.7 45.8 %all-to-all-start = ((bf16[128,4,128]{2,1,0:T(4,128)(2,1)}), bf16[128,4,128]{2,1,0:T(4,128)(2,1)S(1)}, u32[]{:S(2)}, u32[]{:S(2)}) async-start(bf16[128,4,128]{2,1,0:T(4,128)(2,1)} %bitcast.8), calls=%async_computation | async-start | bytes 262144 | tf_op jit(solution)/shard_map/all_to_all | solution.py:407
  35.9 10.1 %collective-permute-start = (bf16[2,72,384]{2,1,0:T(8,128)(2,1)}, bf16[2,72,384]{2,1,0:T(8,128)(2,1)S(1)}, u32[]{:S(2)}, u32[]{:S(2)}) collective-permute-start(bf16[2,72,384]{2,1,0:T(8,128)(2,1)} %get-tuple-element.13), channel_id=1, source_target_pairs={{0,1},{1,2},{2,3},{3,4},{4,5},{5,6},{6,7},{7,8},{8,9},{9,10},{10,1... | collective-permute-start | bytes 331784 | tf_op jit(solution)/shard_map/ppermute | solution.py:405
  36.0 9.9 %collective-permute-start.1 = (bf16[2,72,384]{2,1,0:T(8,128)(2,1)}, bf16[2,72,384]{2,1,0:T(8,128)(2,1)S(1)}, u32[]{:S(2)}, u32[]{:S(2)}) collective-permute-start(bf16[2,72,384]{2,1,0:T(8,128)(2,1)} %get-tuple-element.14), channel_id=1, source_target_pairs={{1,0},{2,1},{3,2},{4,3},{5,4},{6,5},{7,6},{8,7},{9,8},{10,9},{11,1... | collective-permute-start | bytes 331784 | tf_op jit(solution)/shard_map/ppermute | solution.py:406
